TPU v7x, 32 devices: a whole 2x2x4 slice. The times are simulated.
32 devices in a mesh: model: 4 (over z), data: 2 (over y), stage: 4 (over x, core).
Axes of the slice: x: 2, y: 2, z: 4, core: 2. Of those that a mesh axis runs over, the one named last changes fastest.
Arguments:
- w_up: float32 [4, 768, 3072], P('stage', None, 'model')
- w_down: float32 [4, 3072, 768], P('stage', 'model')
- m_up: float32 [4, 768, 3072], P('stage', None, 'model')
- m_down: float32 [4, 3072, 768], P('stage', 'model')
- v_up: float32 [4, 768, 3072], P('stage', None, 'model')
- v_down: float32 [4, 3072, 768], P('stage', 'model')
- g_up: float32 [2, 4, 768, 3072], P('data', 'stage', None, 'model')
- g_down: float32 [2, 4, 3072, 768], P('data', 'stage', 'model')
- acts_last: bfloat16 [4, 2048, 768], P('stage', 'data')
- grad_out: bfloat16 [2048, 768], P('data')
- x_next: bfloat16 [16, 2048, 768], P(None, 'data')
- learn_rate: float32 [1], replicated
- max_norm: float32 [1], replicated
Outputs:
- output 1: float32 [4, 768, 3072], P('stage', None, 'model')
- output 2: float32 [4, 3072, 768], P('stage', 'model')
- output 3: float32 [4, 768, 3072], P('stage', None, 'model')
- output 4: float32 [4, 3072, 768], P('stage', 'model')
- output 5: float32 [4, 768, 3072], P('stage', None, 'model')
- output 6: float32 [4, 3072, 768], P('stage', 'model')
- output 7: bfloat16 [16, 2048, 768], P(None, 'data')
All inputs are finite; a program needn't handle non-finite values.
Results may differ from a plain program's by a relative error of at most 0.00895596.
Values are sent between devices in bfloat16 or wider.
A program may use at most 1 GiB of HBM per device.

v0:
```python
import jax
import jax.numpy as jnp
from jax import lax
from jax.sharding import PartitionSpec as P

ADAM_STEP = 10
BETA_ONE = 0.9
BETA_TWO = 0.95
ADAM_EPS = 1e-8
WEIGHT_DECAY = 0.1
NORM_EPS = 1e-6
CONTRACT_LAST = (((1,), (1,)), ((), ()))
CONTRACT_FIRST = (((0,), (0,)), ((), ()))


def gelu_vjp(pre_act, upstream):
    pull_back = jax.vjp(jax.nn.gelu, pre_act)[1]
    return pull_back(upstream)[0]


def adamw_update(weight, moment_one, moment_two, grad_step, step_rate):
    mom_new = BETA_ONE * moment_one + (1.0 - BETA_ONE) * grad_step
    sec_new = BETA_TWO * moment_two + (1.0 - BETA_TWO) * grad_step * grad_step
    one_corr = 1.0 - BETA_ONE ** ADAM_STEP
    two_corr = 1.0 - BETA_TWO ** ADAM_STEP
    direction = (mom_new / one_corr) / (jnp.sqrt(sec_new / two_corr) + ADAM_EPS)
    weight_new = weight - step_rate * (direction + WEIGHT_DECAY * weight)
    return weight_new, mom_new, sec_new


def solution(mesh):
    n_stage = mesh.shape['stage']
    n_data = mesh.shape['data']
    down_perm = [(sender, sender - 1) for sender in range(1, n_stage)]
    up_perm = [(sender, sender + 1) for sender in range(n_stage - 1)]
    up_spec = P('stage', None, 'model')
    down_spec = P('stage', 'model', None)
    row_spec = P(None, 'data', None)
    in_specs = (up_spec, down_spec, up_spec, down_spec, up_spec, down_spec, P('data', 'stage', None, 'model'), P('data', 'stage', 'model', None), P('stage', 'data', None), P('data', None), row_spec, P(None), P(None))
    out_specs = (up_spec, down_spec, up_spec, down_spec, up_spec, down_spec, row_spec)

    def device_step(w_up, w_down, m_up, m_down, v_up, v_down, g_up, g_down, acts_last, grad_out, x_next, learn_rate, max_norm):
        stage_id = lax.axis_index('stage')
        acts_in = acts_last[0]
        up_bf = w_up[0].astype(jnp.bfloat16)
        down_bf = w_down[0].astype(jnp.bfloat16)
        row_count, d_model = acts_in.shape
        ff_local = up_bf.shape[1]
        n_micro = x_next.shape[0]

        def back_core(upstream):
            pre_act = jnp.dot(acts_in, up_bf, preferred_element_type=jnp.float32)
            hidden = jax.nn.gelu(pre_act).astype(jnp.bfloat16)
            grad_hid = lax.dot_general(upstream, down_bf, CONTRACT_LAST, preferred_element_type=jnp.float32)
            grad_pre = gelu_vjp(pre_act, grad_hid).astype(jnp.bfloat16)
            return hidden, grad_pre

        def back_send(state_in):
            hidden, grad_pre = back_core(state_in[0])
            part_sum = lax.dot_general(grad_pre, up_bf, CONTRACT_LAST, preferred_element_type=jnp.float32)
            return hidden, grad_pre, state_in[0], part_sum

        def hold_send(state_in):
            return state_in[1], state_in[2], state_in[3], jnp.zeros((row_count, d_model), jnp.float32)

        def back_keep(state_in):
            hidden, grad_pre = back_core(state_in[0])
            return hidden, grad_pre, state_in[0]

        def hold_keep(state_in):
            return state_in[1], state_in[2], state_in[3]

        upstream = grad_out
        keep_hid = jnp.zeros((row_count, ff_local), jnp.bfloat16)
        keep_pre = jnp.zeros((row_count, ff_local), jnp.bfloat16)
        keep_up = grad_out
        for step_idx in range(n_stage - 1):
            active = stage_id == n_stage - 1 - step_idx
            keep_hid, keep_pre, keep_up, part_sum = lax.cond(active, back_send, hold_send, (upstream, keep_hid, keep_pre, keep_up))
            summed = lax.psum(part_sum, 'model')
            grad_in = (upstream.astype(jnp.float32) + summed).astype(jnp.bfloat16)
            upstream = lax.ppermute(grad_in, 'stage', down_perm)
        keep_hid, keep_pre, keep_up = lax.cond(stage_id == 0, back_keep, hold_keep, (upstream, keep_hid, keep_pre, keep_up))

        grad_down = lax.dot_general(keep_hid, keep_up, CONTRACT_FIRST, preferred_element_type=jnp.float32)
        grad_up = lax.dot_general(acts_in, keep_pre, CONTRACT_FIRST, preferred_element_type=jnp.float32)
        mean_up = lax.psum(g_up[0, 0] + grad_up, 'data') / n_data
        mean_down = lax.psum(g_down[0, 0] + grad_down, 'data') / n_data
        local_sq = lax.psum(jnp.sum(mean_up * mean_up) + jnp.sum(mean_down * mean_down), 'model')
        norm_acc = local_sq
        for step_idx in range(n_stage - 1):
            incoming = lax.ppermute(norm_acc, 'stage', down_perm)
            norm_acc = jnp.where(stage_id == n_stage - 2 - step_idx, local_sq + incoming, norm_acc)
        clip_cur = jnp.minimum(1.0, max_norm[0] / (jnp.sqrt(norm_acc) + NORM_EPS))
        step_rate = learn_rate[0]

        def apply_update(state_in):
            clip_now = state_in[1]
            up_w, up_m, up_v = adamw_update(w_up[0], m_up[0], v_up[0], clip_now * mean_up, step_rate)
            down_w, down_m, down_v = adamw_update(w_down[0], m_down[0], v_down[0], clip_now * mean_down, step_rate)
            return (up_w, down_w, up_m, down_m, up_v, down_v, up_w.astype(jnp.bfloat16), down_w.astype(jnp.bfloat16))

        def keep_state(state_in):
            return state_in[0]

        def fwd_local(state_in):
            acts_cur, up_new_bf, down_new_bf = state_in
            pre_act = jnp.dot(acts_cur, up_new_bf, preferred_element_type=jnp.float32)
            hidden = jax.nn.gelu(pre_act).astype(jnp.bfloat16)
            return jnp.dot(hidden, down_new_bf, preferred_element_type=jnp.float32)

        def fwd_idle(state_in):
            return jnp.zeros((row_count, d_model), jnp.float32)

        opt_state = (w_up[0], w_down[0], m_up[0], m_down[0], v_up[0], v_down[0], up_bf, down_bf)
        acts_cur = x_next[0]
        finished = []
        for step_idx in range(n_micro + n_stage - 1):
            if step_idx < n_stage:
                opt_state = lax.cond(stage_id == step_idx, apply_update, keep_state, (opt_state, clip_cur))
            if 0 < step_idx < n_micro:
                acts_cur = jnp.where(stage_id == 0, x_next[step_idx], acts_cur)
            micro_idx = step_idx - stage_id
            is_busy = (micro_idx >= 0) & (micro_idx < n_micro)
            branch = lax.cond(is_busy, fwd_local, fwd_idle, (acts_cur, opt_state[6], opt_state[7]))
            summed = lax.psum(branch, 'model')
            acts_out = (acts_cur.astype(jnp.float32) + summed).astype(jnp.bfloat16)
            if step_idx >= n_stage - 1:
                finished.append(acts_out)
            if step_idx < n_micro + n_stage - 2:
                acts_cur = lax.ppermute(acts_out, 'stage', up_perm)
            if step_idx < n_stage - 1:
                clip_cur = lax.ppermute(clip_cur, 'stage', up_perm)
        y_local = jnp.stack(finished)
        y_next = lax.psum(jnp.where(stage_id == n_stage - 1, y_local, jnp.zeros_like(y_local)), 'stage')
        return (opt_state[0][None], opt_state[1][None], opt_state[2][None], opt_state[3][None], opt_state[4][None], opt_state[5][None], y_next)

    return jax.shard_map(device_step, mesh=mesh, in_specs=in_specs, out_specs=out_specs, check_vma=False)
```

profile of v0, /device:TPU:0, one launch (start us, length us, event | category | flops | bytes accessed | tf_op | source)
XLA Modules:
  0.0 4076.7 jit_solution(7115122915479229697)
XLA Ops:
  17.5 129.6 %all-reduce.26.cloned.1.call-done = f32[1024,768]{1,0:T(8,128)} async-done(((f32[1024,768]{1,0:T(8,128)}), f32[1024,768]{1,0:T(8,128)}) %all-reduce.26.cloned.1.call-update) | async-done | bytes 3145744 | tf_op jit(solution)/shard_map/psum | solution.py:80
  158.2 146.4 %all-reduce.28.cloned.1.call-done = f32[1024,768]{1,0:T(8,128)} async-done(((f32[1024,768]{1,0:T(8,128)}), f32[1024,768]{1,0:T(8,128)}) %all-reduce.28.cloned.1.call-update) | async-done | bytes 3145744 | tf_op jit(solution)/shard_map/psum | solution.py:80
  315.8 146.9 %all-reduce.30.cloned.1.call-done = f32[1024,768]{1,0:T(8,128)} async-done(((f32[1024,768]{1,0:T(8,128)}), f32[1024,768]{1,0:T(8,128)}) %all-reduce.30.cloned.1.call-update) | async-done | bytes 3145744 | tf_op jit(solution)/shard_map/psum | solution.py:80
  473.9 10.1 conditional.30
  497.9 117.6 %all-reduce.72.cloned.1.call-done = (f32[768,768]{0,1:T(8,128)}, f32[768,768]{0,1:T(8,128)}) async-done(((f32[768,768]{0,1:T(8,128)}, f32[768,768]{0,1:T(8,128)}), (f32[768,768]{0,1:T(8,128)}, f32[768,768]{0,1:T(8,128)})) %all-reduce.72.cloned.1.call-update) | async-done | bytes 4718608 | tf_op jit(solution)/shard_map/psum | solution.py:87
  623.9 12.2 psum.187
  652.6 19.1 conditional.31
  659.1 12.6 fusion.401
  671.7 6.3 conditional.35
  671.8 6.3 fusion.64
  678.1 116.3 %all-reduce.32.cloned.1.call-done = f32[1024,768]{1,0:T(8,128)} async-done(((f32[1024,768]{1,0:T(8,128)}), f32[1024,768]{1,0:T(8,128)}) %all-reduce.32.cloned.1.call-update) | async-done | bytes 3145744 | tf_op jit(solution)/shard_map/psum | solution.py:126
  813.7 152.1 %all-reduce.34.cloned.1.call-done = f32[1024,768]{1,0:T(8,128)} async-done(((f32[1024,768]{1,0:T(8,128)}), f32[1024,768]{1,0:T(8,128)}) %all-reduce.34.cloned.1.call-update) | async-done | bytes 3145744 | tf_op jit(solution)/shard_map/psum | solution.py:126
  984.9 154.5 %all-reduce.36.cloned.1.call-done = f32[1024,768]{1,0:T(8,128)} async-done(((f32[1024,768]{1,0:T(8,128)}), f32[1024,768]{1,0:T(8,128)}) %all-reduce.36.cloned.1.call-update) | async-done | bytes 3145744 | tf_op jit(solution)/shard_map/psum | solution.py:126
  1160.7 137.4 %all-reduce.38.cloned.1.call-done = f32[1024,768]{1,0:T(8,128)} async-done(((f32[1024,768]{1,0:T(8,128)}), f32[1024,768]{1,0:T(8,128)}) %all-reduce.38.cloned.1.call-update) | async-done | bytes 3145744 | tf_op jit(solution)/shard_map/psum | solution.py:126
  1315.7 136.5 %all-reduce.40.cloned.1.call-done = f32[1024,768]{1,0:T(8,128)} async-done(((f32[1024,768]{1,0:T(8,128)}), f32[1024,768]{1,0:T(8,128)}) %all-reduce.40.cloned.1.call-update) | async-done | bytes 3145744 | tf_op jit(solution)/shard_map/psum | solution.py:126
  1469.9 136.5 %all-reduce.42.cloned.1.call-done = f32[1024,768]{1,0:T(8,128)} async-done(((f32[1024,768]{1,0:T(8,128)}), f32[1024,768]{1,0:T(8,128)}) %all-reduce.42.cloned.1.call-update) | async-done | bytes 3145744 | tf_op jit(solution)/shard_map/psum | solution.py:126
  1624.4 136.1 %all-reduce.44.cloned.1.call-done = f32[1024,768]{1,0:T(8,128)} async-done(((f32[1024,768]{1,0:T(8,128)}), f32[1024,768]{1,0:T(8,128)}) %all-reduce.44.cloned.1.call-update) | async-done | bytes 3145744 | tf_op jit(solution)/shard_map/psum | solution.py:126
  1778.1 136.5 %all-reduce.46.cloned.1.call-done = f32[1024,768]{1,0:T(8,128)} async-done(((f32[1024,768]{1,0:T(8,128)}), f32[1024,768]{1,0:T(8,128)}) %all-reduce.46.cloned.1.call-update) | async-done | bytes 3145744 | tf_op jit(solution)/shard_map/psum | solution.py:126
  1932.3 136.5 %all-reduce.48.cloned.1.call-done = f32[1024,768]{1,0:T(8,128)} async-done(((f32[1024,768]{1,0:T(8,128)}), f32[1024,768]{1,0:T(8,128)}) %all-reduce.48.cloned.1.call-update) | async-done | bytes 3145744 | tf_op jit(solution)/shard_map/psum | solution.py:126
  2086.4 136.5 %all-reduce.50.cloned.1.call-done = f32[1024,768]{1,0:T(8,128)} async-done(((f32[1024,768]{1,0:T(8,128)}), f32[1024,768]{1,0:T(8,128)}) %all-reduce.50.cloned.1.call-update) | async-done | bytes 3145744 | tf_op jit(solution)/shard_map/psum | solution.py:126
  2240.6 136.5 %all-reduce.52.cloned.1.call-done = f32[1024,768]{1,0:T(8,128)} async-done(((f32[1024,768]{1,0:T(8,128)}), f32[1024,768]{1,0:T(8,128)}) %all-reduce.52.cloned.1.call-update) | async-done | bytes 3145744 | tf_op jit(solution)/shard_map/psum | solution.py:126
  2394.7 136.5 %all-reduce.54.cloned.1.call-done = f32[1024,768]{1,0:T(8,128)} async-done(((f32[1024,768]{1,0:T(8,128)}), f32[1024,768]{1,0:T(8,128)}) %all-reduce.54.cloned.1.call-update) | async-done | bytes 3145744 | tf_op jit(solution)/shard_map/psum | solution.py:126
  2548.9 136.5 %all-reduce.56.cloned.1.call-done = f32[1024,768]{1,0:T(8,128)} async-done(((f32[1024,768]{1,0:T(8,128)}), f32[1024,768]{1,0:T(8,128)}) %all-reduce.56.cloned.1.call-update) | async-done | bytes 3145744 | tf_op jit(solution)/shard_map/psum | solution.py:126
  2703.2 136.3 %all-reduce.58.cloned.1.call-done = f32[1024,768]{1,0:T(8,128)} async-done(((f32[1024,768]{1,0:T(8,128)}), f32[1024,768]{1,0:T(8,128)}) %all-reduce.58.cloned.1.call-update) | async-done | bytes 3145744 | tf_op jit(solution)/shard_map/psum | solution.py:126
  2857.1 136.5 %all-reduce.60.cloned.1.call-done = f32[1024,768]{1,0:T(8,128)} async-done(((f32[1024,768]{1,0:T(8,128)}), f32[1024,768]{1,0:T(8,128)}) %all-reduce.60.cloned.1.call-update) | async-done | bytes 3145744 | tf_op jit(solution)/shard_map/psum | solution.py:126
  3011.3 136.5 %all-reduce.62.cloned.1.call-done = f32[1024,768]{1,0:T(8,128)} async-done(((f32[1024,768]{1,0:T(8,128)}), f32[1024,768]{1,0:T(8,128)}) %all-reduce.62.cloned.1.call-update) | async-done | bytes 3145744 | tf_op jit(solution)/shard_map/psum | solution.py:126
  3159.1 142.4 %all-reduce.64.cloned.1.call-done = f32[1024,768]{1,0:T(8,128)} async-done(((f32[1024,768]{1,0:T(8,128)}), f32[1024,768]{1,0:T(8,128)}) %all-reduce.64.cloned.1.call-update) | async-done | bytes 3145744 | tf_op jit(solution)/shard_map/psum | solution.py:126
  3313.1 142.3 %all-reduce.66.cloned.1.call-done = f32[1024,768]{1,0:T(8,128)} async-done(((f32[1024,768]{1,0:T(8,128)}), f32[1024,768]{1,0:T(8,128)}) %all-reduce.66.cloned.1.call-update) | async-done | bytes 3145744 | tf_op jit(solution)/shard_map/psum | solution.py:126
  3466.8 136.5 %all-reduce.68.cloned.1.call-done = f32[1024,768]{1,0:T(8,128)} async-done(((f32[1024,768]{1,0:T(8,128)}), f32[1024,768]{1,0:T(8,128)}) %all-reduce.68.cloned.1.call-update) | async-done | bytes 3145744 | tf_op jit(solution)/shard_map/psum | solution.py:126
  3607.1 9.5 broadcast_select_fusion
  3616.6 432.3 %all-reduce.70.cloned.1.call-done = bf16[16,1024,768]{2,1,0:T(8,128)(2,1)} async-done(((bf16[16,1024,768]{2,1,0:T(8,128)(2,1)}), bf16[16,1024,768]{2,1,0:T(8,128)(2,1)}) %all-reduce.70.cloned.1.call-update) | async-done | bytes 25165840 | tf_op jit(solution)/shard_map/psum | solution.py:135
  4048.9 20.5 copy.211
  (256 shorter events, 488.7 us)
Async XLA Ops:
  7.2 140.0 %all-reduce.26.cloned.1.call-start = ((), (), s32[]{:S(2)}) async-start(), calls=%async_computation | async-start | bytes 6291456 | tf_op jit(solution)/shard_map/psum | solution.py:80
  17.5 287.1 %all-reduce.28.cloned.1.call-start = ((), (), s32[]{:S(2)}) async-start(), calls=%async_computation.1 | async-start | bytes 6291456 | tf_op jit(solution)/shard_map/psum | solution.py:80
  151.0 5.2 collective-permute-start
  158.1 304.6 %all-reduce.30.cloned.1.call-start = ((), (), s32[]{:S(2)}) async-start(), calls=%async_computation.2 | async-start | bytes 6291456 | tf_op jit(solution)/shard_map/psum | solution.py:80
  308.4 5.2 collective-permute-start.1
  315.8 299.8 %all-reduce.72.cloned.1.call-start = ((), (), s32[]{:S(2)}) async-start(), calls=%async_computation.23 | async-start | bytes 9437184 | tf_op jit(solution)/shard_map/psum | solution.py:87
  466.6 7.4 collective-permute-start.2
  494.5 299.8 %all-reduce.32.cloned.1.call-start = ((), (), s32[]{:S(2)}) async-start(), calls=%async_computation.3 | async-start | bytes 6291456 | tf_op jit(solution)/shard_map/psum | solution.py:126
  646.4 4.9 collective-permute-start.5
  678.0 287.7 %all-reduce.34.cloned.1.call-start = ((), (), s32[]{:S(2)}) async-start(), calls=%async_computation.4 | async-start | bytes 6291456 | tf_op jit(solution)/shard_map/psum | solution.py:126
  798.2 6.2 collective-permute-start.9
  813.4 326.0 %all-reduce.36.cloned.1.call-start = ((), (), s32[]{:S(2)}) async-start(), calls=%async_computation.5 | async-start | bytes 6291456 | tf_op jit(solution)/shard_map/psum | solution.py:126
  969.6 6.2 collective-permute-start.10
  984.9 313.1 %all-reduce.38.cloned.1.call-start = ((), (), s32[]{:S(2)}) async-start(), calls=%async_computation.6 | async-start | bytes 6291456 | tf_op jit(solution)/shard_map/psum | solution.py:126
  1143.4 6.4 collective-permute-start.11
  1160.6 291.6 %all-reduce.40.cloned.1.call-start = ((), (), s32[]{:S(2)}) async-start(), calls=%async_computation.7 | async-start | bytes 6291456 | tf_op jit(solution)/shard_map/psum | solution.py:126
  1315.7 290.7 %all-reduce.42.cloned.1.call-start = ((), (), s32[]{:S(2)}) async-start(), calls=%async_computation.8 | async-start | bytes 6291456 | tf_op jit(solution)/shard_map/psum | solution.py:126
  1469.8 290.7 %all-reduce.44.cloned.1.call-start = ((), (), s32[]{:S(2)}) async-start(), calls=%async_computation.9 | async-start | bytes 6291456 | tf_op jit(solution)/shard_map/psum | solution.py:126
  1624.0 290.7 %all-reduce.46.cloned.1.call-start = ((), (), s32[]{:S(2)}) async-start(), calls=%async_computation.10 | async-start | bytes 6291456 | tf_op jit(solution)/shard_map/psum | solution.py:126
  1778.1 290.7 %all-reduce.48.cloned.1.call-start = ((), (), s32[]{:S(2)}) async-start(), calls=%async_computation.11 | async-start | bytes 6291456 | tf_op jit(solution)/shard_map/psum | solution.py:126
  1932.2 290.7 %all-reduce.50.cloned.1.call-start = ((), (), s32[]{:S(2)}) async-start(), calls=%async_computation.12 | async-start | bytes 6291456 | tf_op jit(solution)/shard_map/psum | solution.py:126
  2072.6 4.3 collective-permute-start.17
  2086.4 290.7 %all-reduce.52.cloned.1.call-start = ((), (), s32[]{:S(2)}) async-start(), calls=%async_computation.13 | async-start | bytes 6291456 | tf_op jit(solution)/shard_map/psum | solution.py:126
  2240.5 290.7 %all-reduce.54.cloned.1.call-start = ((), (), s32[]{:S(2)}) async-start(), calls=%async_computation.14 | async-start | bytes 6291456 | tf_op jit(solution)/shard_map/psum | solution.py:126
  2394.7 290.7 %all-reduce.56.cloned.1.call-start = ((), (), s32[]{:S(2)}) async-start(), calls=%async_computation.15 | async-start | bytes 6291456 | tf_op jit(solution)/shard_map/psum | solution.py:126
  2548.8 290.7 %all-reduce.58.cloned.1.call-start = ((), (), s32[]{:S(2)}) async-start(), calls=%async_computation.16 | async-start | bytes 6291456 | tf_op jit(solution)/shard_map/psum | solution.py:126
  2703.0 290.7 %all-reduce.60.cloned.1.call-start = ((), (), s32[]{:S(2)}) async-start(), calls=%async_computation.17 | async-start | bytes 6291456 | tf_op jit(solution)/shard_map/psum | solution.py:126
  2857.1 290.7 %all-reduce.62.cloned.1.call-start = ((), (), s32[]{:S(2)}) async-start(), calls=%async_computation.18 | async-start | bytes 6291456 | tf_op jit(solution)/shard_map/psum | solution.py:126
  3011.2 290.2 %all-reduce.64.cloned.1.call-start = ((), (), s32[]{:S(2)}) async-start(), calls=%async_computation.19 | async-start | bytes 6291456 | tf_op jit(solution)/shard_map/psum | solution.py:126
  3159.1 296.4 %all-reduce.66.cloned.1.call-start = ((), (), s32[]{:S(2)}) async-start(), calls=%async_computation.20 | async-start | bytes 6291456 | tf_op jit(solution)/shard_map/psum | solution.py:126
  3313.1 290.2 %all-reduce.68.cloned.1.call-start = ((), (), s32[]{:S(2)}) async-start(), calls=%async_computation.21 | async-start | bytes 6291456 | tf_op jit(solution)/shard_map/psum | solution.py:126
  3466.8 582.2 %all-reduce.70.cloned.1.call-start = ((), (), s32[]{:S(2)}) async-start(), calls=%async_computation.22 | async-start | bytes 50331648 | tf_op jit(solution)/shard_map/psum | solution.py:135
  (47 other events, 135.6 us)
Sparse Core Ops, SparseCore 0:
  17.6 129.5 all-reduce.25
  158.3 146.2 all-reduce.27
  315.9 146.8 all-reduce.29
  494.7 120.8 all-reduce.71
  678.2 116.1 all-reduce.31
  813.6 152.1 all-reduce.33
  985.0 154.3 all-reduce.35
  1160.7 137.2 all-reduce.37
  1315.8 136.3 all-reduce.39
  1469.9 136.3 all-reduce.41
  1624.1 136.3 all-reduce.43
  1778.2 136.3 all-reduce.45
  1932.4 136.3 all-reduce.47
  2086.5 136.3 all-reduce.49
  2240.6 136.3 all-reduce.51
  2394.8 136.3 all-reduce.53
  2548.9 136.3 all-reduce.55
  2703.1 136.3 all-reduce.57
  2857.2 136.3 all-reduce.59
  3011.4 136.3 all-reduce.61
  3159.2 142.2 all-reduce.63
  3313.2 142.2 all-reduce.65
  3466.9 136.3 all-reduce.67
  3616.7 432.1 all-reduce.69
where the time goes:
time: 4090 us; the launch traced here: 4080 us
  waiting for transfers between devices  3650 us (89%)
  other arithmetic  158 us (4%)
  matrix products  101 us (2%)
  local copies, waits for them, and re-layouts  81.7 us (2%)
  starting transfers between devices  49.1 us (1%)
    psum x19, waiting for transfers between devices, device_step(): summed = lax.psum(branch, 'model')  2620 us
    psum x1, waiting for transfers between devices, device_step(): lax.psum(jnp.where(stage_id == n_stage - 1, y_local, jnp.zeros_like(y_loc...  432 us
    psum x3, waiting for transfers between devices, device_step(): summed = lax.psum(part_sum, 'model')  423 us
    psum x1, waiting for transfers between devices, device_step(): mean_up = lax.psum(g_up[0, 0] + grad_up, 'data') / n_data  118 us
    dot_general x16, matrix products, fwd_local(): return jnp.dot(hidden, down_new_bf, preferred_element_type=jnp.float32)  83 us
  transfers between devices with their start and end apart: 51, of which 46 were waited for; matrix products, arithmetic and copies ran while one was open for 0% of the time, Pallas kernels for 0%

commit v1 on v0

v1 whole, which is shorter than its diff:
```python
import functools

import jax
import jax.numpy as jnp
from jax import lax
from jax.experimental import pallas as pl
from jax.experimental.pallas import tpu as pltpu
from jax.sharding import PartitionSpec as P

ADAM_STEP = 10
BETA_ONE = 0.9
BETA_TWO = 0.95
ADAM_EPS = 1e-8
WEIGHT_DECAY = 0.1
NORM_EPS = 1e-6
CONTRACT_LAST = (((1,), (1,)), ((), ()))
CONTRACT_FIRST = (((0,), (0,)), ((), ()))
F32 = jnp.float32
BF16 = jnp.bfloat16


def gelu_vjp(pre_act, upstream):
    pull_back = jax.vjp(jax.nn.gelu, pre_act)[1]
    return pull_back(upstream)[0]


def adamw_update(weight, moment_one, moment_two, grad_step, step_rate):
    mom_new = BETA_ONE * moment_one + (1.0 - BETA_ONE) * grad_step
    sec_new = BETA_TWO * moment_two + (1.0 - BETA_TWO) * grad_step * grad_step
    one_corr = 1.0 - BETA_ONE ** ADAM_STEP
    two_corr = 1.0 - BETA_TWO ** ADAM_STEP
    direction = (mom_new / one_corr) / (jnp.sqrt(sec_new / two_corr) + ADAM_EPS)
    weight_new = weight - step_rate * (direction + WEIGHT_DECAY * weight)
    return weight_new, mom_new, sec_new


def dot(left, right, dims=None):
    if dims is None:
        return jnp.dot(left, right, preferred_element_type=F32)
    return lax.dot_general(left, right, dims, preferred_element_type=F32)


class Net:
    def __init__(self):
        self.z = lax.axis_index('model')
        self.y = lax.axis_index('data')
        self.s = lax.axis_index('stage')
        self.y_other = 1 - self.y
        self.s_across = lax.rem(self.s + 2, 4)
        self.s_sibling = self.s + 1 - 2 * lax.rem(self.s, 2)
        self.sends = []

    def send(self, src, dst, send_sem, recv_sem, to):
        return pltpu.make_async_remote_copy(src_ref=src, dst_ref=dst, send_sem=send_sem, recv_sem=recv_sem, device_id=to, device_id_type=pl.DeviceIdType.MESH)


def when_all(conds, body):
    cond = None
    for c in conds:
        if c is not None:
            cond = c if cond is None else cond & c
    if cond is None:
        body()
    else:
        pl.when(cond)(body)


def side_of(z, n_model, d, side):
    if d == 0:
        return z, None
    if side == 0:
        return lax.max(z - d, 0), z - d >= 0
    return lax.min(z + d, n_model - 1), z + d < n_model


def chain_kernel(n_model, own, acts, grad, gathered, wfull, pre, gbuf, obuf, wsend, wrecv, ysend, yrecv, gsend, grecv, csend, crecv):
    net = Net()
    z, y, s = net.z, net.y, net.s
    n_stage = 4
    half, width = own.shape[2], own.shape[3]
    pend = []

    def z_copy(zs, mat, up, src):
        to = z + 1 if up else z - 1
        return net.send(src, wfull.at[zs, y, mat], wsend.at[int(up), zs, mat], wrecv.at[zs, mat], {'model': to})

    def y_copy(zs, mat):
        return net.send(wfull.at[zs, y, mat], wfull.at[zs, y, mat], ysend.at[zs, mat], yrecv.at[zs, mat], {'data': net.y_other})

    for mat in range(2):
        own_half = own.at[mat, y]
        for up in (False, True):
            cond = (z < n_model - 1) if up else (z > 0)
            def start(mat=mat, up=up, own_half=own_half):
                z_copy(z, mat, up, own_half).start()
            pl.when(cond)(start)
    for mat in range(2):
        for h in range(2):
            wfull[z, h, mat] = own[mat, h]

    def use(zs, mat):
        return wfull.at[zs, :, mat]

    for d in range(1, n_model):
        for mat in range(2):
            for side in range(2):
                zs, ok = side_of(z, n_model, d, side)
                up = side == 0
                room = (z < n_model - 1) if up else (z > 0)
                def take(zs=zs, mat=mat, up=up):
                    z_copy(zs, mat, up, wfull.at[zs, y, mat]).wait_recv()
                    y_copy(zs, mat).start()
                when_all([ok], take)
                def forward(zs=zs, mat=mat, up=up):
                    z_copy(zs, mat, up, wfull.at[zs, y, mat]).start()
                when_all([ok, room], forward)
    for d in range(1, n_model):
        for mat in range(2):
            for side in range(2):
                zs, ok = side_of(z, n_model, d, side)
                def take_y(zs=zs, mat=mat):
                    net.send(wfull.at[zs, net.y_other, mat], wfull.at[zs, net.y_other, mat], ysend.at[zs, mat], yrecv.at[zs, mat], {'data': net.y_other}).wait_recv()
                when_all([ok], take_y)

    def pre_body(j, _):
        up_w = wfull[j, :, 0].reshape(2 * half, width)
        pre[j] = dot(acts[...], up_w)
        return 0

    lax.fori_loop(0, n_model, pre_body, 0)

    g_in = net.send(obuf, gbuf, csend.at[0], crecv.at[0], {'stage': lax.max(s - 1, 0)})

    def g_copy(zs, up, src):
        to = z + 1 if up else z - 1
        return net.send(src, gathered.at[zs], gsend.at[int(up), zs], grecv.at[zs], {'model': to})

    @pl.when(s == n_stage - 1)
    def _():
        gbuf[...] = grad[...]

    @pl.when(s < n_stage - 1)
    def _():
        g_in.wait_recv()
        for up in (False, True):
            cond = (z < n_model - 1) if up else (z > 0)
            def start(up=up):
                g_copy(z, up, gbuf).start()
            pl.when(cond)(start)

    @pl.when(s > 0)
    def _():
        def back_body(j, total):
            down_w = wfull[j, :, 1].reshape(2 * half, width)
            up_w = wfull[j, :, 0].reshape(2 * half, width)
            grad_hid = dot(gbuf[...], down_w, CONTRACT_LAST)
            grad_pre = gelu_back(pre[j], grad_hid).astype(BF16)
            return total + dot(grad_pre, up_w, CONTRACT_LAST)

        total = lax.fori_loop(0, n_model, back_body, jnp.zeros(gbuf.shape, F32))
        obuf[...] = (gbuf[...].astype(F32) + total).astype(BF16)
        g_in.start()

    gathered[z] = gbuf[...]

    @pl.when(s < n_stage - 1)
    def _():
        for d in range(1, n_model):
            for side in range(2):
                zs, ok = side_of(z, n_model, d, side)
                up = side == 0
                room = (z < n_model - 1) if up else (z > 0)
                def take(zs=zs, up=up):
                    g_copy(zs, up, gathered.at[zs]).wait_recv()
                when_all([ok], take)
                def forward(zs=zs, up=up):
                    g_copy(zs, up, gathered.at[zs]).start()
                when_all([ok, room], forward)

    for d in range(n_model):
        for side in range(2 if d else 1):
            zs, ok = side_of(z, n_model, d, side)
            for up in (False, True):
                if d and up != (side == 0):
                    continue
                room = (z < n_model - 1) if up else (z > 0)
                for mat in range(2):
                    def drain(zs=zs, up=up, mat=mat):
                        z_copy(zs, mat, up, wfull.at[zs, y, mat]).wait_send()
                    when_all([ok, room], drain)
                def drain_g(zs=zs, up=up):
                    g_copy(zs, up, gathered.at[zs]).wait_send()
                when_all([ok, room, s < n_stage - 1], drain_g)
            if d:
                for mat in range(2):
                    def drain_y(zs=zs, mat=mat):
                        y_copy(zs, mat).wait_send()
                    when_all([ok], drain_y)

    @pl.when(s > 0)
    def _():
        g_in.wait_send()


def gelu_back(pre_act, upstream):
    scale = 0.7978845608028654
    cubic = 0.044715
    inner = scale * (pre_act + cubic * pre_act * pre_act * pre_act)
    tanh = jnp.tanh(inner)
    slope = scale * (1.0 + 3.0 * cubic * pre_act * pre_act)
    return upstream * (0.5 * (1.0 + tanh) + 0.5 * pre_act * (1.0 - tanh * tanh) * slope)


VMEM_SPEC = pl.BlockSpec(memory_space=pltpu.VMEM)
ANY_SPEC = pl.BlockSpec(memory_space=pl.ANY)
DMA = pltpu.SemaphoreType.DMA


def backward_rows(own, acts, grad, n_model):
    rows, width = acts.shape
    half = own.shape[2]
    return pl.pallas_call(
        functools.partial(chain_kernel, n_model),
        out_shape=jax.ShapeDtypeStruct((n_model, rows, width), BF16),
        in_specs=[VMEM_SPEC] * 3,
        out_specs=VMEM_SPEC,
        scratch_shapes=[
            pltpu.VMEM((n_model, 2, 2, half, width), BF16),
            pltpu.VMEM((n_model, rows, 2 * half), F32),
            pltpu.VMEM((rows, width), BF16),
            pltpu.VMEM((rows, width), BF16),
            DMA((2, n_model, 2)), DMA((n_model, 2)), DMA((n_model, 2)), DMA((n_model, 2)),
            DMA((2, n_model)), DMA((n_model,)), DMA((1,)), DMA((1,)),
        ],
        compiler_params=pltpu.CompilerParams(has_side_effects=True, vmem_limit_bytes=48 * 1024 * 1024),
        name='chain',
    )(own, acts, grad)


def weights_kernel(n_model, own, new, zsend, xsend, ysend, csend, recv, local):
    net = Net()
    z, y, s = net.z, net.y, net.s
    c = lax.rem(s, 2)

    def slot(ss, zs, ys, mat):
        return new.at[ss, zs, ys, mat]

    def copy(src, ss, zs, ys, mat, sem, to):
        return net.send(src, slot(ss, zs, ys, mat), sem, recv.at[ss, zs, ys, mat], to)

    def go(kind, ss, zs, ys, mat, src=None):
        src = slot(ss, zs, ys, mat) if src is None else src
        if kind == 'up':
            return copy(src, ss, zs, ys, mat, zsend.at[1, zs, mat], {'model': z + 1})
        if kind == 'down':
            return copy(src, ss, zs, ys, mat, zsend.at[0, zs, mat], {'model': z - 1})
        if kind == 'x':
            return copy(src, ss, zs, ys, mat, xsend.at[zs, ys, mat], {'stage': net.s_across})
        if kind == 'y':
            return copy(src, ss, zs, ys, mat, ysend.at[ss // 2, zs, mat], {'data': net.y_other})
        return copy(src, ss, zs, ys, mat, csend.at[ss // 2, zs, ys, mat], {'stage': net.s_sibling})

    def arrive(ss, zs, ys, mat):
        go('c', ss, zs, ys, mat).wait_recv()

    def first(d, side, mat, act):
        zs, ok = side_of(z, n_model, d, side)
        src = own.at[mat] if d == 0 else None
        for kind in ('up', 'down'):
            if d and kind != ('up' if side == 0 else 'down'):
                continue
            room = (z < n_model - 1) if kind == 'up' else (z > 0)
            when_all([ok, room], lambda kind=kind: act(go(kind, s, zs, y, mat, src)))
        def rest():
            for kind in ('x', 'y', 'c'):
                act(go(kind, s, zs, y, mat, src))
        when_all([ok], rest)

    def beside(mat, zs):
        return (s, zs, net.y_other, mat) if mat == 0 else (net.s_across, zs, y, mat)

    def second(d, side, mat, act):
        zs, ok = side_of(z, n_model, d, side)
        ss, ys, kind = (net.s_across, y, 'y') if mat == 0 else (s, net.y_other, 'x')
        def rest():
            act(go(kind, ss, zs, ys, mat))
            act(go('c', ss, zs, ys, mat))
            act(go('c', *beside(mat, zs)))
        when_all([ok], rest)

    def third(d, side, mat, act):
        zs, ok = side_of(z, n_model, d, side)
        when_all([ok], lambda: act(go('c', net.s_across, zs, net.y_other, mat)))

    def start(copy):
        copy.start()

    def end(copy):
        copy.wait_send()

    def step(level, d):
        for side in range(2 if d else 1):
            for mat in range(2):
                zs, ok = side_of(z, n_model, d, side)
                if level == 0:
                    if d:
                        when_all([ok], lambda: arrive(s, zs, y, mat))
                    first(d, side, mat, start)
                elif level == 1:
                    ss, ys = (net.s_across, y) if mat == 0 else (s, net.y_other)
                    def both():
                        arrive(ss, zs, ys, mat)
                        arrive(*beside(mat, zs))
                    when_all([ok], both)
                    second(d, side, mat, start)
                else:
                    when_all([ok], lambda: arrive(net.s_across, zs, net.y_other, mat))
                    third(d, side, mat, start)

    mine = pltpu.make_async_copy(own, new.at[s, z, y], local.at[0])
    mine.start()
    for level, d in ((0, 0), (0, 1), (1, 0), (0, 2), (1, 1), (2, 0), (0, 3), (1, 2), (2, 1), (1, 3), (2, 2), (2, 3)):
        step(level, d)
    for ss in (net.s_sibling, lax.rem(net.s_sibling + 2, 4)):
        for zs in range(n_model):
            for ys in range(2):
                for mat in range(2):
                    arrive(ss, zs, ys, mat)
    for d in range(n_model):
        for side in range(2 if d else 1):
            for mat in range(2):
                first(d, side, mat, end)
                second(d, side, mat, end)
                third(d, side, mat, end)
    mine.wait()


def gather_weights(own, n_stage, n_model, n_data):
    n_mat, half, width = own.shape
    return pl.pallas_call(
        functools.partial(weights_kernel, n_model),
        out_shape=jax.ShapeDtypeStruct((n_stage, n_model, n_data, n_mat, half, width), BF16),
        in_specs=[VMEM_SPEC],
        out_specs=ANY_SPEC,
        scratch_shapes=[
            DMA((2, n_model, 2)), DMA((n_model, 2, 2)), DMA((2, n_model, 2)), DMA((2, n_model, 2, 2)),
            DMA((n_stage, n_model, n_data, n_mat)), DMA((1,)),
        ],
        compiler_params=pltpu.CompilerParams(has_side_effects=True),
        name='weights',
    )(own)


def out_kernel(n_model, cut, own, out, zsend, xsend, csend, recv, local):
    net = Net()
    z, s = net.z, net.s
    rows = own.shape[0]
    parts = (pl.ds(0, cut), pl.ds(cut, rows - cut))

    def slot(ss, zs, part):
        return out.at[ss * n_model + zs, parts[part]]

    def go(kind, ss, zs, part, src=None):
        src = slot(ss, zs, part) if src is None else src
        if kind == 'up':
            sem, to = zsend.at[1, ss // 2, zs, part], {'model': z + 1}
        elif kind == 'down':
            sem, to = zsend.at[0, ss // 2, zs, part], {'model': z - 1}
        elif kind == 'x':
            sem, to = xsend.at[zs, part], {'stage': net.s_across}
        else:
            sem, to = csend.at[ss // 2, zs, part], {'stage': net.s_sibling}
        return net.send(src, slot(ss, zs, part), sem, recv.at[ss, zs, part], to)

    def arrive(ss, zs, part):
        go('c', ss, zs, part).wait_recv()

    def along_z(ss, d, side, part, act, src=None):
        zs, ok = side_of(z, n_model, d, side)
        for kind in ('up', 'down'):
            if d and kind != ('up' if side == 0 else 'down'):
                continue
            room = (z < n_model - 1) if kind == 'up' else (z > 0)
            when_all([ok, room], lambda kind=kind: act(go(kind, ss, zs, part, src)))

    def big(d, side, act):
        zs, ok = side_of(z, n_model, d, side)
        src = own.at[parts[0]] if d == 0 else None
        along_z(s, d, side, 0, act, src)
        def rest():
            act(go('x', s, zs, 0, src))
            act(go('c', s, zs, 0, src))
        when_all([ok], rest)

    def big_across(d, side, act):
        zs, ok = side_of(z, n_model, d, side)
        when_all([ok], lambda: act(go('c', net.s_across, zs, 0)))

    def small(ss, d, side, act, src=None):
        zs, ok = side_of(z, n_model, d, side)
        along_z(ss, d, side, 1, act, src)
        when_all([ok], lambda: act(go('c', ss, zs, 1, src)))

    def start(copy):
        copy.start()

    def end(copy):
        copy.wait_send()

    def sides(d):
        return range(2 if d else 1)

    mine = pltpu.make_async_copy(own, out.at[s * n_model + z], local.at[0])
    mine.start()
    go('x', s, z, 1, own.at[parts[1]]).start()
    big(0, 0, start)
    small(s, 0, 0, start, own.at[parts[1]])
    arrive(net.s_across, z, 1)
    small(net.s_across, 0, 0, start)
    for d in range(1, n_model):
        for side in sides(d):
            zs, ok = side_of(z, n_model, d, side)
            when_all([ok], lambda: arrive(s, zs, 0))
            big(d, side, start)
        for ss in (s, net.s_across):
            for side in sides(d):
                zs, ok = side_of(z, n_model, d, side)
                when_all([ok], lambda: arrive(ss, zs, 1))
                small(ss, d, side, start)
        for side in sides(d - 1):
            zs, ok = side_of(z, n_model, d - 1, side)
            when_all([ok], lambda: arrive(net.s_across, zs, 0))
            big_across(d - 1, side, start)
    for side in sides(n_model - 1):
        zs, ok = side_of(z, n_model, n_model - 1, side)
        when_all([ok], lambda: arrive(net.s_across, zs, 0))
        big_across(n_model - 1, side, start)
    for ss in (net.s_sibling, lax.rem(net.s_sibling + 2, 4)):
        for zs in range(n_model):
            for part in range(2):
                arrive(ss, zs, part)
    go('x', s, z, 1, own.at[parts[1]]).wait_send()
    for d in range(n_model):
        for side in sides(d):
            big(d, side, end)
            big_across(d, side, end)
            small(s, d, side, end, own.at[parts[1]] if d == 0 else None)
            small(net.s_across, d, side, end)
    mine.wait()


def gather_out(own, n_stage, n_model):
    rows, width = own.shape
    cut = rows * 7 // 8
    return pl.pallas_call(
        functools.partial(out_kernel, n_model, cut),
        out_shape=jax.ShapeDtypeStruct((n_stage * n_model, rows, width), BF16),
        in_specs=[VMEM_SPEC],
        out_specs=ANY_SPEC,
        scratch_shapes=[
            DMA((2, 2, n_model, 2)), DMA((n_model, 2)), DMA((2, n_model, 2)),
            DMA((n_stage, n_model, 2)), DMA((1,)),
        ],
        compiler_params=pltpu.CompilerParams(has_side_effects=True),
        name='gather_out',
    )(own)


def norm_kernel(n_stage, n_data, n_model, part, total, slots, send_sem, recv_sem):
    net = Net()
    z, y, s = net.z, net.y, net.s
    count = n_stage * n_data * n_model
    me = (s * n_data + y) * n_model + z

    def copy(k):
        other = lax.rem(me + k, count)
        to = {'model': lax.rem(other, n_model), 'data': lax.rem(other // n_model, n_data), 'stage': other // (n_model * n_data)}
        return net.send(part, slots.at[me], send_sem.at[k], recv_sem.at[me], to)

    def from_other(k):
        other = lax.rem(me + k, count)
        return net.send(part, slots.at[other], send_sem.at[k], recv_sem.at[other], {'model': z, 'data': y, 'stage': lax.rem(s + 1, n_stage)})

    for k in range(1, count):
        copy(k).start()
    slots[me] = part[...]
    for k in range(1, count):
        from_other(k).wait_recv()
    total[...] = jnp.sum(slots[...], axis=0)
    for k in range(1, count):
        copy(k).wait_send()


def total_sum(part, n_stage, n_data, n_model):
    count = n_stage * n_data * n_model
    tile = pl.pallas_call(
        functools.partial(norm_kernel, n_stage, n_data, n_model),
        out_shape=jax.ShapeDtypeStruct((8, 128), F32),
        in_specs=[VMEM_SPEC],
        out_specs=VMEM_SPEC,
        scratch_shapes=[pltpu.VMEM((count, 8, 128), F32), DMA((count,)), DMA((count,))],
        compiler_params=pltpu.CompilerParams(has_side_effects=True),
        name='norm',
    )(part)
    return jnp.sum(tile)


def mlp_kernel(rows_step, acts, up, down, out, cur, total):
    p, j = pl.program_id(0), pl.program_id(1)
    rows, width = cur.shape

    @pl.when((p == 0) & (j == 0))
    def _():
        cur[...] = acts[...]

    up_w = up[0, 0, :, 0].reshape(width, width)
    down_w = down[0, 0, :, 0].reshape(width, width)
    for r in range(rows // rows_step):
        at = pl.ds(r * rows_step, rows_step)
        hid = jax.nn.gelu(dot(cur[at, :], up_w)).astype(BF16)
        part = dot(hid, down_w)

        @pl.when(j == 0)
        def _():
            total[at, :] = part

        @pl.when(j > 0)
        def _():
            total[at, :] += part

    @pl.when(j == pl.num_programs(1) - 1)
    def _():
        cur[...] = (cur[...].astype(F32) + total[...]).astype(BF16)

    @pl.when((p == pl.num_programs(0) - 1) & (j == pl.num_programs(1) - 1))
    def _():
        out[...] = cur[...]


def forward_rows(acts, new):
    n_stage, n_model, n_data, _, half, width = new.shape
    rows = acts.shape[0]
    def spec(mat):
        return pl.BlockSpec((1, 1, n_data, 1, half, width), lambda p, j: (p, j, 0, mat, 0, 0))
    whole = pl.BlockSpec((rows, width), lambda p, j: (0, 0))
    return pl.pallas_call(
        functools.partial(mlp_kernel, 256),
        out_shape=jax.ShapeDtypeStruct((rows, width), BF16),
        grid=(n_stage, n_model),
        in_specs=[whole, spec(0), spec(1)],
        out_specs=whole,
        scratch_shapes=[pltpu.VMEM((rows, width), BF16), pltpu.VMEM((rows, width), F32)],
        compiler_params=pltpu.CompilerParams(dimension_semantics=('arbitrary', 'arbitrary'), vmem_limit_bytes=40 * 1024 * 1024),
        cost_estimate=pl.CostEstimate(flops=4 * n_stage * rows * width * width * n_model, bytes_accessed=2 * new.size, transcendentals=n_stage * n_model * rows * width),
        name='forward',
    )(acts, new, new)


def solution(mesh):
    n_stage = mesh.shape['stage']
    n_data = mesh.shape['data']
    n_model = mesh.shape['model']
    swap = [(0, 1), (1, 0)]
    up_spec = P('stage', None, 'model')
    down_spec = P('stage', 'model', None)
    row_spec = P(None, 'data', None)
    in_specs = (up_spec, down_spec, up_spec, down_spec, up_spec, down_spec, P('data', 'stage', None, 'model'), P('data', 'stage', 'model', None), P('stage', 'data', None), P('data', None), row_spec, P(None), P(None))
    out_specs = (up_spec, down_spec, up_spec, down_spec, up_spec, down_spec, row_spec)

    def device_step(w_up, w_down, m_up, m_down, v_up, v_down, g_up, g_down, acts_last, grad_out, x_next, learn_rate, max_norm):
        stage_id = lax.axis_index('stage')
        model_id = lax.axis_index('model')
        data_id = lax.axis_index('data')
        acts_in = acts_last[0]
        w_up, w_down, m_up, m_down, v_up, v_down = (t[0] for t in (w_up, w_down, m_up, m_down, v_up, v_down))
        g_up, g_down = g_up[0, 0], g_down[0, 0]
        d_model, ff_local = w_up.shape
        rows = acts_in.shape[0]
        row_part = rows // n_model
        half = d_model // n_data
        up_bf = w_up.astype(BF16)
        down_bf = w_down.astype(BF16)

        def half_of(arr, which):
            return lax.dynamic_slice_in_dim(arr, which * half, half, 0)

        own = jnp.stack([up_bf, down_bf]).reshape(2, n_data, half, d_model)
        acts_part = lax.dynamic_slice_in_dim(acts_in, model_id * row_part, row_part, 0)
        grad_part = lax.dynamic_slice_in_dim(grad_out, model_id * row_part, row_part, 0)
        gathered = backward_rows(own, acts_part, grad_part, n_model).reshape(rows, d_model)
        grad_full = jnp.where(stage_id == n_stage - 1, grad_out, gathered)

        pre_act = dot(acts_in, up_bf)
        hidden = jax.nn.gelu(pre_act).astype(BF16)
        grad_hid = dot(grad_full, down_bf, CONTRACT_LAST)
        grad_pre = gelu_vjp(pre_act, grad_hid).astype(BF16)
        sum_up = g_up + dot(acts_in, grad_pre, CONTRACT_FIRST)
        sum_down = g_down + dot(hidden, grad_full, CONTRACT_FIRST)
        got_up = lax.ppermute(half_of(sum_up, 1 - data_id), 'data', swap)
        got_down = lax.ppermute(half_of(sum_down, 1 - data_id), 'data', swap)
        mean_up = (half_of(sum_up, data_id) + got_up) / n_data
        mean_down = (half_of(sum_down, data_id) + got_down) / n_data
        sq = mean_up * mean_up + mean_down * mean_down
        norm_sq = total_sum(jnp.sum(sq.reshape(-1, 8, d_model // 128, 128), axis=(0, 2)), n_stage, n_data, n_model)
        clip = jnp.minimum(1.0, max_norm[0] / (jnp.sqrt(norm_sq) + NORM_EPS))
        step_rate = learn_rate[0]

        up_half = adamw_update(half_of(w_up, data_id), half_of(m_up, data_id), half_of(v_up, data_id), clip * mean_up, step_rate)[0]
        down_half = adamw_update(half_of(w_down, data_id), half_of(m_down, data_id), half_of(v_down, data_id), clip * mean_down, step_rate)[0]
        new = gather_weights(jnp.stack([up_half.astype(BF16), down_half.astype(BF16)]), n_stage, n_model, n_data)

        other_up = lax.ppermute(mean_up, 'data', swap)
        other_down = lax.ppermute(mean_down, 'data', swap)

        def join(mine, other):
            first = jnp.where(data_id == 0, mine, other)
            second = jnp.where(data_id == 0, other, mine)
            return jnp.concatenate([first, second], axis=0)

        up_w, up_m, up_v = adamw_update(w_up, m_up, v_up, clip * join(mean_up, other_up), step_rate)
        down_w, down_m, down_v = adamw_update(w_down, m_down, v_down, clip * join(mean_down, other_down), step_rate)

        acts_cur = lax.dynamic_index_in_dim(x_next, stage_id * n_model + model_id, 0, keepdims=False)
        y_next = gather_out(forward_rows(acts_cur, new), n_stage, n_model)
        return (up_w[None], down_w[None], up_m[None], down_m[None], up_v[None], down_v[None], y_next)

    return jax.shard_map(device_step, mesh=mesh, in_specs=in_specs, out_specs=out_specs, check_vma=False)
```

time: 4090 us -> 668 us (0.16)
  waiting for transfers between devices: 3650 us -> 35.5 us
  Pallas kernels: 0 us -> 541 us
  other arithmetic: 158 us -> 31.8 us
  matrix products: 101 us -> 18.2 us
  local copies, waits for them, and re-layouts: 81.7 us -> 34.1 us
  starting transfers between devices: 49.1 us -> 4.11 us
    psum x24 -> x0, waiting for transfers between devices: 3590 us -> none  [the longest x19 2620 us: device_step(): summed = lax.psum(branch, 'model')]
    pallas_call x0 -> x5, Pallas kernels: none -> 541 us  [the longest x1 162 us: gather_weights(): pl.pallas_call(functools.partial(weights_kernel, n_model), out_shape=jax....]
    dot_general x20 -> x3, matrix products: 101 us -> 18.2 us  [the longest x2 13.9 us: dot(): return lax.dot_general(left, right, dims, preferred_element_type=F32)]
    unnamed x15 -> x0, other arithmetic: 57.9 us -> none
    select_n x16 -> x1, other arithmetic: 51.6 us -> 1.41 us  [device_step(): grad_full = jnp.where(stage_id == n_stage - 1, grad_out, gathered)]
    ppermute x27 -> x4, starting transfers between devices: 47.3 us -> 4.11 us  [the longest x1 1.41 us: device_step(): got_down = lax.ppermute(half_of(sum_down, 1 - data_id), 'data', swap)]
  transfers between devices with their start and end apart: 51 -> 4, of which waited for: 46 -> 2; matrix products, arithmetic and copies ran while one was open for 0% -> 1% of each run, Pallas kernels for 0% -> 32%
where the time goes in v1:
time: 668 us; the launch traced here: 667 us
  Pallas kernels  541 us (81%)
  waiting for transfers between devices  35.5 us (5%)
  local copies, waits for them, and re-layouts  34.1 us (5%)
  other arithmetic  31.8 us (5%)
  matrix products  18.2 us (3%)
    pallas_call x1, Pallas kernels, gather_weights(): pl.pallas_call(functools.partial(weights_kernel, n_model), out_shape=jax....  162 us
    pallas_call x1, Pallas kernels, backward_rows(): pl.pallas_call(functools.partial(chain_kernel, n_model), out_shape=jax.Sh...  151 us
    pallas_call x1, Pallas kernels, gather_out(): pl.pallas_call(functools.partial(out_kernel, n_model, cut), out_shape=jax...  149 us
    pallas_call x1, Pallas kernels, forward_rows(): pl.pallas_call(functools.partial(mlp_kernel, 256), out_shape=jax.ShapeDty...  67.2 us
    unnamed x29, local copies, waits for them, and re-layouts  27.7 us
    ppermute x1, waiting for transfers between devices, device_step(): got_down = lax.ppermute(half_of(sum_down, 1 - data_id), 'data', swap)  18.6 us
    ppermute x1, waiting for transfers between devices, device_step(): got_up = lax.ppermute(half_of(sum_up, 1 - data_id), 'data', swap)  16.8 us
    dot_general x2, matrix products, dot(): return lax.dot_general(left, right, dims, preferred_element_type=F32)  13.9 us
  transfers between devices with their start and end apart: 4, of which 2 were waited for; matrix products, arithmetic and copies ran while one was open for 1% of the time, Pallas kernels for 32%

profile of v1, /device:TPU:0, one launch (start us, length us, event | category | flops | bytes accessed | tf_op | source)
XLA Modules:
  0.0 667.3 jit_solution(2759935840666489384)
XLA Ops:
  0.7 1.1 constant_dynamic-slice_fusion.2.grad
  2.2 2.9 convert_element_type.26
  5.3 4.3 fusion.11
  9.6 2.9 pad_maximum_fusion.own
  12.5 1.7 copy-done.2
  14.2 150.5 %chain.1 = bf16[4,256,768]{2,1,0:T(8,128)(2,1)S(1)} custom-call(bf16[2,2,384,768]{3,2,1,0:T(8,128)(2,1)S(1)} %copy-done.2, bf16[256,768]{1,0:T(8,128)(2,1)S(1)} %dynamic-slice_bitcast_fusion.1.acts, bf16[256,768]{1,0:T(8,128)(2,1)S(1)} %constant_dynamic-slice_fusion.2.grad), custom_call_target="tpu_custom_call" | custom-call | tf_op jit(solution)/shard_map/chain/pallas_call | solution.py:222
  164.7 1.4 bitcast_select_fusion
  166.1 9.4 %bitcast_add_fusion.1 = f32[768,768]{1,0:T(8,128)} fusion(f32[1,1,768,768]{3,2,1,0:T(8,128)} %param.19, bf16[1,1024,768]{2,1,0:T(8,128)(2,1)S(1)} %copy-done, f32[1024,768]{1,0:T(8,128)} %fusion.11, bf16[1024,768]{1,0:T(8,128)(2,1)} %bitcast_select_fusion, bf16[1,768,768]{2,1,0:T(8,128)(2,1)S(1)} %convert_element_type.27), kind=kOutput, calls=%fused_computation.18 | convolution fusion | flops 2432237568 | bytes 12189696 | tf_op jit(solution)/shard_map/dot_general | solution.py:40
  175.5 2.5 constant_dynamic-slice_fusion.1
  178.6 4.5 bitcast_add_fusion
  183.1 1.4 copy-done.9
  184.5 1.1 constant_dynamic-slice_fusion
  185.6 1.4 collective-permute-start.1
  188.3 1.7 dynamic-slice_bitcast_fusion.acts
  190.0 16.8 %collective-permute-done = f32[384,768]{1,0:T(8,128)S(1)} collective-permute-done((f32[384,768]{1,0:T(8,128)}, f32[384,768]{1,0:T(8,128)S(1)}, u32[]{:S(2)}, u32[]{:S(2)}) %collective-permute-start) | collective-permute-done | bytes 1179680 | tf_op jit(solution)/shard_map/ppermute | solution.py:599
  206.8 1.0 copy-done.11
  207.8 18.6 %collective-permute-done.1 = f32[384,768]{1,0:T(8,128)} collective-permute-done((f32[384,768]{1,0:T(8,128)}, f32[384,768]{1,0:T(8,128)}, u32[]{:S(2)}, u32[]{:S(2)}) %collective-permute-start.1) | collective-permute-done | bytes 1179680 | tf_op jit(solution)/shard_map/ppermute | solution.py:600
  226.5 4.0 bitcast_reduce_fusion
  230.5 12.0 %norm.1 = f32[8,128]{1,0:T(8,128)} custom-call(f32[8,128]{1,0:T(8,128)} %get-tuple-element.13.part), custom_call_target="tpu_custom_call" | custom-call | tf_op jit(solution)/shard_map/norm/pallas_call | solution.py:496
  242.6 1.3 reduce_sum.19
  244.6 6.5 fusion.46
  251.1 1.1 pad_maximum_fusion.1.own
  252.2 161.9 %weights.1.up.down = bf16[4,4,2,2,384,768]{5,4,3,2,1,0:T(8,128)(2,1)} custom-call(bf16[2,384,768]{2,1,0:T(8,128)(2,1)} %pad_maximum_fusion.1.own), custom_call_target="tpu_custom_call" | custom-call | tf_op jit(solution)/shard_map/weights/pallas_call | solution.py:340
  414.8 1.4 collective-permute-start.3
  416.2 67.2 %forward.1.own = bf16[1024,768]{1,0:T(8,128)(2,1)S(1)} custom-call(bf16[1024,768]{1,0:T(8,128)(2,1)S(1)} %dynamic-slice_bitcast_fusion.acts, bf16[4,4,2,2,384,768]{5,4,3,2,1,0:T(8,128)(2,1)} %weights.1.up.down, bf16[4,4,2,2,384,768]{5,4,3,2,1,0:T(8,128)(2,1)} %weights.1.up.down), custom_call_target="tpu_custom_call" | custom-call | flops 38654705664 | bytes 37748736 | tf_op jit(solution)/shard_map/forward/pallas_call | solution.py:546
  483.4 1.1 copy-done.3
  484.6 149.0 %gather_out.1 = bf16[16,1024,768]{2,1,0:T(8,128)(2,1)} custom-call(bf16[1024,768]{1,0:T(8,128)(2,1)} %copy-done.3), custom_call_target="tpu_custom_call" | custom-call | tf_op jit(solution)/shard_map/gather_out/pallas_call | solution.py:455
  633.6 1.9 select_bitcast_fusion.3
  635.6 1.6 select_bitcast_fusion.1
  637.2 0.8 copy-done.5
  638.7 8.0 %multiply_subtract_fusion = (f32[1,768,768]{2,1,0:T(8,128)}, f32[1,768,768]{2,1,0:T(8,128)}, f32[1,768,768]{2,1,0:T(8,128)}, f32[1,768,768]{2,1,0:T(8,128)}, f32[1,768,768]{2,1,0:T(8,128)}, /*index=5*/f32[1,768,768]{2,1,0:T(8,128)}) fusion(f32[1,768,768]{2,1,0:T(8,128)S(1)} %copy-done.5, f32[]{:T(128)} %bitcast.101, ...), kind=kLoop, calls=%fused_computation.19 | loop fusion | flops 20054016 | bytes 33030152 | tf_op jit(solution)/shard_map/sub | solution.py:33
  646.7 20.6 %copy.23 = bf16[16,1024,768]{2,1,0:T(8,128)(2,1)} copy(bf16[16,1024,768]{2,1,0:T(8,128)(2,1)} %gather_out.1) | data formatting | bytes 50331648
  (29 shorter events, 2.5 us)
Async XLA Ops:
  0.6 1.5 copy-start
  2.2 3.0 copy-start.4
  12.5 1.7 copy-start.2
  14.2 150.5 %copy-start.12 = (bf16[1024,768]{1,0:T(8,128)(2,1)S(1)}, bf16[1024,768]{1,0:T(8,128)(2,1)}, u32[]{:S(2)}) copy-start(bf16[1024,768]{1,0:T(8,128)(2,1)} %param.22) | copy-start | bytes 4718596
  175.5 3.1 copy-start.13
  178.0 28.8 %collective-permute-start = (f32[384,768]{1,0:T(8,128)}, f32[384,768]{1,0:T(8,128)S(1)}, u32[]{:S(2)}, u32[]{:S(2)}) collective-permute-start(f32[384,768]{1,0:T(8,128)} %constant_dynamic-slice_fusion.1), channel_id=1, source_target_pairs={{0,4},{4,0},{1,5},{5,1},{2,6},{6,2},{3,7},{7,3},{8,12},{12,8},{9,1... | collective-permute-start | bytes 3538952 | tf_op jit(solution)/shard_map/ppermute | solution.py:599
  183.1 1.4 copy-start.9
  185.6 40.9 %collective-permute-start.1 = (f32[384,768]{1,0:T(8,128)}, f32[384,768]{1,0:T(8,128)}, u32[]{:S(2)}, u32[]{:S(2)}) collective-permute-start(f32[384,768]{1,0:T(8,128)} %constant_dynamic-slice_fusion), channel_id=1, source_target_pairs={{0,4},{4,0},{1,5},{5,1},{2,6},{6,2},{3,7},{7,3},{8,12},{12,8},{9,1... | collective-permute-start | bytes 3538952 | tf_op jit(solution)/shard_map/ppermute | solution.py:600
  188.3 38.1 %copy-start.10 = (f32[768,768]{1,0:T(8,128)S(1)}, f32[768,768]{1,0:T(8,128)}, u32[]{:S(2)}) copy-start(f32[768,768]{1,0:T(8,128)} %copy-done.9) | copy-start | bytes 7077892
  206.8 1.0 copy-start.11
  414.1 219.5 %collective-permute-start.2 = (f32[384,768]{1,0:T(8,128)}, f32[384,768]{1,0:T(8,128)}, u32[]{:S(2)}, u32[]{:S(2)}) collective-permute-start(f32[384,768]{1,0:T(8,128)} %get-tuple-element.15), channel_id=1, source_target_pairs={{0,4},{4,0},{1,5},{5,1},{2,6},{6,2},{3,7},{7,3},{8,12},{12,8},{9,1... | collective-permute-start | bytes 3538952 | tf_op jit(solution)/shard_map/ppermute | solution.py:612
  414.8 220.8 %collective-permute-start.3 = (f32[384,768]{1,0:T(8,128)S(1)}, f32[384,768]{1,0:T(8,128)}, u32[]{:S(2)}, u32[]{:S(2)}) collective-permute-start(f32[384,768]{1,0:T(8,128)S(1)} %get-tuple-element.14), channel_id=1, source_target_pairs={{0,4},{4,0},{1,5},{5,1},{2,6},{6,2},{3,7},{7,3},{8,12},{12,8},{9,1... | collective-permute-start | bytes 3538952 | tf_op jit(solution)/shard_map/ppermute | solution.py:613
  483.4 1.1 copy-start.3
  633.6 3.6 copy-start.7
  633.6 3.6 copy-start.8
  635.6 2.4 copy-start.5
  635.6 3.1 copy-start.6
  646.7 20.6 %copy-start.1 = (bf16[1,1024,768]{2,1,0:T(8,128)(2,1)S(1)}, bf16[1,1024,768]{2,1,0:T(8,128)(2,1)}, u32[]{:S(2)}) copy-start(bf16[1,1024,768]{2,1,0:T(8,128)(2,1)} %param.21) | copy-start | bytes 4718596

commit v2 on v1

v2 whole, which is shorter than its diff:
```python
import functools

import jax
import jax.numpy as jnp
from jax import lax
from jax.experimental import pallas as pl
from jax.experimental.pallas import tpu as pltpu
from jax.sharding import PartitionSpec as P

ADAM_STEP = 10
BETA_ONE = 0.9
BETA_TWO = 0.95
ADAM_EPS = 1e-8
WEIGHT_DECAY = 0.1
NORM_EPS = 1e-6
CONTRACT_LAST = (((1,), (1,)), ((), ()))
CONTRACT_FIRST = (((0,), (0,)), ((), ()))
F32 = jnp.float32
BF16 = jnp.bfloat16


def adamw_update(weight, moment_one, moment_two, grad_step, step_rate):
    mom_new = BETA_ONE * moment_one + (1.0 - BETA_ONE) * grad_step
    sec_new = BETA_TWO * moment_two + (1.0 - BETA_TWO) * grad_step * grad_step
    one_corr = 1.0 - BETA_ONE ** ADAM_STEP
    two_corr = 1.0 - BETA_TWO ** ADAM_STEP
    direction = (mom_new / one_corr) / (jnp.sqrt(sec_new / two_corr) + ADAM_EPS)
    weight_new = weight - step_rate * (direction + WEIGHT_DECAY * weight)
    return weight_new, mom_new, sec_new


def dot(left, right, dims=None):
    if dims is None:
        return jnp.dot(left, right, preferred_element_type=F32)
    return lax.dot_general(left, right, dims, preferred_element_type=F32)


class Net:
    def __init__(self):
        self.z = lax.axis_index('model')
        self.y = lax.axis_index('data')
        self.s = lax.axis_index('stage')
        self.y_other = 1 - self.y
        self.s_across = lax.rem(self.s + 2, 4)
        self.s_sibling = self.s + 1 - 2 * lax.rem(self.s, 2)
        self.sends = []

    def send(self, src, dst, send_sem, recv_sem, to):
        return pltpu.make_async_remote_copy(src_ref=src, dst_ref=dst, send_sem=send_sem, recv_sem=recv_sem, device_id=to, device_id_type=pl.DeviceIdType.MESH)


def when_all(conds, body):
    cond = None
    for c in conds:
        if c is not None:
            cond = c if cond is None else cond & c
    if cond is None:
        body()
    else:
        pl.when(cond)(body)


def side_of(z, n_model, d, side):
    if d == 0:
        return z, None
    if side == 0:
        return lax.max(z - d, 0), z - d >= 0
    return lax.min(z + d, n_model - 1), z + d < n_model


def gelu_parts(pre_act):
    scale = 0.7978845608028654
    cubic = 0.044715
    square = pre_act * pre_act
    tanh = jnp.tanh(pre_act * (scale + scale * cubic * square))
    cdf = 0.5 + 0.5 * tanh
    slope = cdf + 0.5 * pre_act * (1.0 - tanh * tanh) * (scale + 3.0 * scale * cubic * square)
    return pre_act * cdf, slope


def chain_kernel(n_stage, n_data, n_model, own, acts, grad, g_up, g_down, mean, norm, wfull, slopes, gbuf, obuf, gathered, hid, slope, dz, sbuf, rbuf, part, slots,
                 wsend, wrecv, ysend, yrecv, gsend, grecv, csend, crecv, rsend, rrecv, nsend, nrecv):
    net = Net()
    z, y, s = net.z, net.y, net.s
    half, width = own.shape[2], own.shape[3]
    few = gbuf.shape[0]

    def z_copy(zs, mat, up, src):
        to = z + 1 if up else z - 1
        return net.send(src, wfull.at[zs, y, mat], wsend.at[int(up), zs, mat], wrecv.at[zs, mat], {'model': to})

    def y_copy(zs, mat, ys):
        return net.send(wfull.at[zs, ys, mat], wfull.at[zs, ys, mat], ysend.at[zs, mat], yrecv.at[zs, mat], {'data': net.y_other})

    def has_room(up):
        return (z < n_model - 1) if up else (z > 0)

    for mat in range(2):
        for up in (False, True):
            when_all([has_room(up)], lambda: z_copy(z, mat, up, own.at[mat, y]).start())
    for mat in range(2):
        for h in range(2):
            wfull[z, h, mat] = own[mat, h]

    up_own = own[0].reshape(2 * half, width)
    down_own = own[1].reshape(2 * half, width)

    def rows_at(k):
        return pl.ds(pl.multiple_of(k * few, few), few)

    def local_body(k, _):
        value, lean = gelu_parts(dot(acts[rows_at(k), :], own[0].reshape(2 * half, width)))
        hid[rows_at(k), :] = value.astype(BF16)
        slope[rows_at(k), :] = lean
        return 0

    lax.fori_loop(0, n_model, local_body, 0)

    for d in range(1, n_model):
        for mat in range(2):
            for side in range(2):
                zs, ok = side_of(z, n_model, d, side)
                up = side == 0
                def take():
                    z_copy(zs, mat, up, wfull.at[zs, y, mat]).wait_recv()
                    y_copy(zs, mat, y).start()
                when_all([ok], take)
                when_all([ok, has_room(up)], lambda: z_copy(zs, mat, up, wfull.at[zs, y, mat]).start())
    for d in range(1, n_model):
        for mat in range(2):
            for side in range(2):
                zs, ok = side_of(z, n_model, d, side)
                when_all([ok], lambda: y_copy(zs, mat, net.y_other).wait_recv())

    def pre_body(j, _):
        slopes[j] = gelu_parts(dot(acts[rows_at(z), :], wfull[j, :, 0].reshape(2 * half, width)))[1]
        return 0

    lax.fori_loop(0, n_model, pre_body, 0)

    g_in = net.send(obuf, gbuf, csend.at[0], crecv.at[0], {'stage': lax.max(s - 1, 0)})

    def g_copy(zs, up, src):
        to = z + 1 if up else z - 1
        return net.send(src, gathered.at[zs], gsend.at[int(up), zs], grecv.at[zs], {'model': to})

    @pl.when(s == n_stage - 1)
    def _():
        gbuf[...] = grad[rows_at(z), :]

    @pl.when(s < n_stage - 1)
    def _():
        g_in.wait_recv()
        for up in (False, True):
            when_all([has_room(up)], lambda: g_copy(z, up, gbuf).start())

    @pl.when(s > 0)
    def _():
        def back_body(j, total):
            grad_hid = dot(gbuf[...], wfull[j, :, 1].reshape(2 * half, width), CONTRACT_LAST)
            grad_pre = (grad_hid * slopes[j]).astype(BF16)
            return total + dot(grad_pre, wfull[j, :, 0].reshape(2 * half, width), CONTRACT_LAST)

        total = lax.fori_loop(0, n_model, back_body, jnp.zeros(gbuf.shape, F32))
        obuf[...] = (gbuf[...].astype(F32) + total).astype(BF16)
        g_in.start()

    @pl.when(s == n_stage - 1)
    def _():
        for k in range(n_model):
            gathered[k] = grad[k * few:(k + 1) * few, :]

    @pl.when(s < n_stage - 1)
    def _():
        gathered[z] = gbuf[...]
        for d in range(1, n_model):
            for side in range(2):
                zs, ok = side_of(z, n_model, d, side)
                up = side == 0
                when_all([ok], lambda: g_copy(zs, up, gathered.at[zs]).wait_recv())
                when_all([ok, has_room(up)], lambda: g_copy(zs, up, gathered.at[zs]).start())

    def dz_body(k, _):
        grad_hid = dot(gathered[k], own[1].reshape(2 * half, width), CONTRACT_LAST)
        dz[rows_at(k), :] = (grad_hid * slope[rows_at(k), :]).astype(BF16)
        return 0

    lax.fori_loop(0, n_model, dz_body, 0)
    grad_all = gathered[...].reshape(n_model * few, width)

    def half_grad(mat, ys):
        at = pl.ds(pl.multiple_of(ys * half, half), half)
        if mat == 0:
            return g_up[at, :] + dot(acts[:, at], dz[...], CONTRACT_FIRST)
        return g_down[at, :] + dot(hid[:, at], grad_all, CONTRACT_FIRST)

    def swap(mat):
        return net.send(sbuf.at[mat], rbuf.at[mat], rsend.at[mat], rrecv.at[mat], {'data': net.y_other})

    for mat in range(2):
        sbuf[mat] = half_grad(mat, net.y_other)
        swap(mat).start()
    for mat in range(2):
        mean[mat] = half_grad(mat, y)
    tile = jnp.zeros((8, 128), F32)
    for mat in range(2):
        swap(mat).wait_recv()
        both = (mean[mat] + rbuf[mat]) / n_data
        mean[mat] = both
        rowsum = jnp.sum((both * both).reshape(half // 8, 8, width), axis=0)
        for k in range(width // 128):
            tile = tile + rowsum[:, k * 128:(k + 1) * 128]

    count = n_stage * n_data * n_model
    me = (s * n_data + y) * n_model + z
    part[...] = tile

    def tell(k):
        other = lax.rem(me + k, count)
        to = {'model': lax.rem(other, n_model), 'data': lax.rem(other // n_model, n_data), 'stage': other // (n_model * n_data)}
        return net.send(part, slots.at[me], nsend.at[k], nrecv.at[me], to)

    def hear(k):
        other = lax.rem(me + k, count)
        return net.send(part, slots.at[other], nsend.at[k], nrecv.at[other], {'data': net.y_other})

    for k in range(1, count):
        tell(k).start()
    slots[me] = tile
    for k in range(1, count):
        hear(k).wait_recv()
    norm[...] = jnp.sum(slots[...], axis=0)

    for k in range(1, count):
        tell(k).wait_send()
    for mat in range(2):
        swap(mat).wait_send()
    for d in range(n_model):
        for side in range(2 if d else 1):
            zs, ok = side_of(z, n_model, d, side)
            for up in (False, True):
                if d and up != (side == 0):
                    continue
                for mat in range(2):
                    when_all([ok, has_room(up)], lambda: z_copy(zs, mat, up, wfull.at[zs, y, mat]).wait_send())
                when_all([ok, has_room(up), s < n_stage - 1], lambda: g_copy(zs, up, gathered.at[zs]).wait_send())
            if d:
                for mat in range(2):
                    when_all([ok], lambda: y_copy(zs, mat, y).wait_send())

    @pl.when(s > 0)
    def _():
        g_in.wait_send()


VMEM_SPEC = pl.BlockSpec(memory_space=pltpu.VMEM)
ANY_SPEC = pl.BlockSpec(memory_space=pl.ANY)
DMA = pltpu.SemaphoreType.DMA


def backward_all(own, acts, grad, g_up, g_down, n_stage, n_data, n_model):
    rows, width = acts.shape
    half = own.shape[2]
    few = rows // n_model
    count = n_stage * n_data * n_model
    return pl.pallas_call(
        functools.partial(chain_kernel, n_stage, n_data, n_model),
        out_shape=(jax.ShapeDtypeStruct((2, half, width), F32), jax.ShapeDtypeStruct((8, 128), F32)),
        in_specs=[VMEM_SPEC] * 5,
        out_specs=(VMEM_SPEC, VMEM_SPEC),
        scratch_shapes=[
            pltpu.VMEM((n_model, 2, 2, half, width), BF16),
            pltpu.VMEM((n_model, few, 2 * half), F32),
            pltpu.VMEM((few, width), BF16),
            pltpu.VMEM((few, width), BF16),
            pltpu.VMEM((n_model, few, width), BF16),
            pltpu.VMEM((rows, 2 * half), BF16),
            pltpu.VMEM((rows, 2 * half), F32),
            pltpu.VMEM((rows, 2 * half), BF16),
            pltpu.VMEM((2, half, width), F32),
            pltpu.VMEM((2, half, width), F32),
            pltpu.VMEM((8, 128), F32),
            pltpu.VMEM((count, 8, 128), F32),
            DMA((2, n_model, 2)), DMA((n_model, 2)), DMA((n_model, 2)), DMA((n_model, 2)),
            DMA((2, n_model)), DMA((n_model,)), DMA((1,)), DMA((1,)), DMA((2,)), DMA((2,)), DMA((count,)), DMA((count,)),
        ],
        compiler_params=pltpu.CompilerParams(has_side_effects=True, vmem_limit_bytes=60 * 1024 * 1024),
        name='backward',
    )(own, acts, grad, g_up, g_down)


def weights_kernel(n_model, own, new, zsend, xsend, ysend, csend, recv, local):
    net = Net()
    z, y, s = net.z, net.y, net.s
    c = lax.rem(s, 2)

    def slot(ss, zs, ys, mat):
        return new.at[ss, zs, ys, mat]

    def copy(src, ss, zs, ys, mat, sem, to):
        return net.send(src, slot(ss, zs, ys, mat), sem, recv.at[ss, zs, ys, mat], to)

    def go(kind, ss, zs, ys, mat, src=None):
        src = slot(ss, zs, ys, mat) if src is None else src
        if kind == 'up':
            return copy(src, ss, zs, ys, mat, zsend.at[1, zs, mat], {'model': z + 1})
        if kind == 'down':
            return copy(src, ss, zs, ys, mat, zsend.at[0, zs, mat], {'model': z - 1})
        if kind == 'x':
            return copy(src, ss, zs, ys, mat, xsend.at[zs, ys, mat], {'stage': net.s_across})
        if kind == 'y':
            return copy(src, ss, zs, ys, mat, ysend.at[ss // 2, zs, mat], {'data': net.y_other})
        return copy(src, ss, zs, ys, mat, csend.at[ss // 2, zs, ys, mat], {'stage': net.s_sibling})

    def arrive(ss, zs, ys, mat):
        go('c', ss, zs, ys, mat).wait_recv()

    def first(d, side, mat, act):
        zs, ok = side_of(z, n_model, d, side)
        src = own.at[mat] if d == 0 else None
        for kind in ('up', 'down'):
            if d and kind != ('up' if side == 0 else 'down'):
                continue
            room = (z < n_model - 1) if kind == 'up' else (z > 0)
            when_all([ok, room], lambda kind=kind: act(go(kind, s, zs, y, mat, src)))
        def rest():
            for kind in ('x', 'y', 'c'):
                act(go(kind, s, zs, y, mat, src))
        when_all([ok], rest)

    def beside(mat, zs):
        return (s, zs, net.y_other, mat) if mat == 0 else (net.s_across, zs, y, mat)

    def second(d, side, mat, act):
        zs, ok = side_of(z, n_model, d, side)
        ss, ys, kind = (net.s_across, y, 'y') if mat == 0 else (s, net.y_other, 'x')
        def rest():
            act(go(kind, ss, zs, ys, mat))
            act(go('c', ss, zs, ys, mat))
            act(go('c', *beside(mat, zs)))
        when_all([ok], rest)

    def third(d, side, mat, act):
        zs, ok = side_of(z, n_model, d, side)
        when_all([ok], lambda: act(go('c', net.s_across, zs, net.y_other, mat)))

    def start(copy):
        copy.start()

    def end(copy):
        copy.wait_send()

    def step(level, d):
        for side in range(2 if d else 1):
            for mat in range(2):
                zs, ok = side_of(z, n_model, d, side)
                if level == 0:
                    if d:
                        when_all([ok], lambda: arrive(s, zs, y, mat))
                    first(d, side, mat, start)
                elif level == 1:
                    ss, ys = (net.s_across, y) if mat == 0 else (s, net.y_other)
                    def both():
                        arrive(ss, zs, ys, mat)
                        arrive(*beside(mat, zs))
                    when_all([ok], both)
                    second(d, side, mat, start)
                else:
                    when_all([ok], lambda: arrive(net.s_across, zs, net.y_other, mat))
                    third(d, side, mat, start)

    mine = pltpu.make_async_copy(own, new.at[s, z, y], local.at[0])
    mine.start()
    for level, d in ((0, 0), (0, 1), (1, 0), (0, 2), (1, 1), (2, 0), (0, 3), (1, 2), (2, 1), (1, 3), (2, 2), (2, 3)):
        step(level, d)
    for ss in (net.s_sibling, lax.rem(net.s_sibling + 2, 4)):
        for zs in range(n_model):
            for ys in range(2):
                for mat in range(2):
                    arrive(ss, zs, ys, mat)
    for d in range(n_model):
        for side in range(2 if d else 1):
            for mat in range(2):
                first(d, side, mat, end)
                second(d, side, mat, end)
                third(d, side, mat, end)
    mine.wait()


def gather_weights(own, n_stage, n_model, n_data):
    n_mat, half, width = own.shape
    return pl.pallas_call(
        functools.partial(weights_kernel, n_model),
        out_shape=jax.ShapeDtypeStruct((n_stage, n_model, n_data, n_mat, half, width), BF16),
        in_specs=[VMEM_SPEC],
        out_specs=ANY_SPEC,
        scratch_shapes=[
            DMA((2, n_model, 2)), DMA((n_model, 2, 2)), DMA((2, n_model, 2)), DMA((2, n_model, 2, 2)),
            DMA((n_stage, n_model, n_data, n_mat)), DMA((1,)),
        ],
        compiler_params=pltpu.CompilerParams(has_side_effects=True),
        name='weights',
    )(own)


def out_kernel(n_model, pieces, own, out, zsend, xsend, csend, recv, local):
    net = Net()
    z, s = net.z, net.s
    last = len(pieces) - 1
    parts = [pl.ds(*piece) for piece in pieces]

    def slot(ss, zs, part):
        return out.at[ss * n_model + zs, parts[part]]

    def go(kind, ss, zs, part, src=None):
        src = slot(ss, zs, part) if src is None else src
        if kind == 'up':
            sem, to = zsend.at[1, ss // 2, zs, part], {'model': z + 1}
        elif kind == 'down':
            sem, to = zsend.at[0, ss // 2, zs, part], {'model': z - 1}
        elif kind == 'x':
            sem, to = xsend.at[zs, part], {'stage': net.s_across}
        else:
            sem, to = csend.at[ss // 2, zs, part], {'stage': net.s_sibling}
        return net.send(src, slot(ss, zs, part), sem, recv.at[ss, zs, part], to)

    def arrive(ss, zs, part):
        go('c', ss, zs, part).wait_recv()

    def source(ss, d, part):
        return own.at[parts[part]] if d == 0 and ss is s else None

    def pass_on(ss, d, side, part, act):
        zs, ok = side_of(z, n_model, d, side)
        src = source(ss, d, part)
        for kind in ('up', 'down'):
            if d and kind != ('up' if side == 0 else 'down'):
                continue
            room = (z < n_model - 1) if kind == 'up' else (z > 0)
            when_all([ok, room], lambda: act(go(kind, ss, zs, part, src)))
        def rest():
            if part < last:
                act(go('x', ss, zs, part, src))
            act(go('c', ss, zs, part, src))
        when_all([ok], rest)

    def across(d, side, part, act):
        zs, ok = side_of(z, n_model, d, side)
        when_all([ok], lambda: act(go('c', net.s_across, zs, part)))

    def start(copy):
        copy.start()

    def end(copy):
        copy.wait_send()

    def sides(d):
        return range(2 if d else 1)

    def take_across(d):
        for part in range(last):
            for side in sides(d):
                zs, ok = side_of(z, n_model, d, side)
                when_all([ok], lambda: arrive(net.s_across, zs, part))
                across(d, side, part, start)

    mine = pltpu.make_async_copy(own, out.at[s * n_model + z], local.at[0])
    mine.start()
    first = go('x', s, z, last, own.at[parts[last]])
    first.start()
    for part in range(last + 1):
        pass_on(s, 0, 0, part, start)
    arrive(net.s_across, z, last)
    pass_on(net.s_across, 0, 0, last, start)
    for d in range(1, n_model):
        for part in range(last):
            for side in sides(d):
                zs, ok = side_of(z, n_model, d, side)
                when_all([ok], lambda: arrive(s, zs, part))
                pass_on(s, d, side, part, start)
        for ss in (s, net.s_across):
            for side in sides(d):
                zs, ok = side_of(z, n_model, d, side)
                when_all([ok], lambda: arrive(ss, zs, last))
                pass_on(ss, d, side, last, start)
        take_across(d - 1)
    take_across(n_model - 1)
    for ss in (net.s_sibling, lax.rem(net.s_sibling + 2, 4)):
        for zs in range(n_model):
            for part in range(last + 1):
                arrive(ss, zs, part)
    first.wait_send()
    for d in range(n_model):
        for side in sides(d):
            for part in range(last + 1):
                pass_on(s, d, side, part, end)
            for part in range(last):
                across(d, side, part, end)
            pass_on(net.s_across, d, side, last, end)
    mine.wait()


def gather_out(own, n_stage, n_model):
    rows, width = own.shape
    unit = rows // 64
    pieces = ((0, 19 * unit), (19 * unit, 19 * unit), (38 * unit, 18 * unit), (56 * unit, 8 * unit))
    n_part = len(pieces)
    return pl.pallas_call(
        functools.partial(out_kernel, n_model, pieces),
        out_shape=jax.ShapeDtypeStruct((n_stage * n_model, rows, width), BF16),
        in_specs=[VMEM_SPEC],
        out_specs=ANY_SPEC,
        scratch_shapes=[
            DMA((2, 2, n_model, n_part)), DMA((n_model, n_part)), DMA((2, n_model, n_part)),
            DMA((n_stage, n_model, n_part)), DMA((1,)),
        ],
        compiler_params=pltpu.CompilerParams(has_side_effects=True, vmem_limit_bytes=4 * 1024 * 1024),
        name='gather_out',
    )(own)


def store_kernel(src, dst, sems):
    n_copy = sems.shape[0]
    step = src.shape[0] // n_copy
    copies = [pltpu.make_async_copy(src.at[pl.ds(k * step, step)], dst.at[pl.ds(k * step, step)], sems.at[k]) for k in range(n_copy)]
    for copy in copies:
        copy.start()
    for copy in copies:
        copy.wait()


def store_out(rows):
    return pl.pallas_call(
        store_kernel,
        out_shape=jax.ShapeDtypeStruct(rows.shape, rows.dtype),
        in_specs=[VMEM_SPEC],
        out_specs=ANY_SPEC,
        scratch_shapes=[DMA((8,))],
        compiler_params=pltpu.CompilerParams(vmem_limit_bytes=4 * 1024 * 1024),
        name='store_out',
    )(rows)


def mlp_kernel(rows_step, acts, up, down, out, cur, total):
    p, j = pl.program_id(0), pl.program_id(1)
    rows, width = cur.shape

    @pl.when((p == 0) & (j == 0))
    def _():
        cur[...] = acts[...]

    @pl.when(j == 0)
    def _():
        total[...] = jnp.zeros(total.shape, F32)

    up_w = up[0, 0, :, 0].reshape(width, width)
    down_w = down[0, 0, :, 0].reshape(width, width)
    n_step = rows // rows_step

    def at(r):
        return pl.ds(r * rows_step, rows_step)

    ahead = dot(cur[at(0), :], up_w)
    for r in range(n_step):
        pre = ahead
        if r + 1 < n_step:
            ahead = dot(cur[at(r + 1), :], up_w)
        total[at(r), :] += dot(gelu_parts(pre)[0].astype(BF16), down_w)

    @pl.when(j == pl.num_programs(1) - 1)
    def _():
        cur[...] = (cur[...].astype(F32) + total[...]).astype(BF16)

    @pl.when((p == pl.num_programs(0) - 1) & (j == pl.num_programs(1) - 1))
    def _():
        out[...] = cur[...]


def forward_rows(acts, new):
    n_stage, n_model, n_data, _, half, width = new.shape
    rows = acts.shape[0]
    def spec(mat):
        return pl.BlockSpec((1, 1, n_data, 1, half, width), lambda p, j: (p, j, 0, mat, 0, 0))
    whole = pl.BlockSpec((rows, width), lambda p, j: (0, 0))
    return pl.pallas_call(
        functools.partial(mlp_kernel, 256),
        out_shape=jax.ShapeDtypeStruct((rows, width), BF16),
        grid=(n_stage, n_model),
        in_specs=[whole, spec(0), spec(1)],
        out_specs=whole,
        scratch_shapes=[pltpu.VMEM((rows, width), BF16), pltpu.VMEM((rows, width), F32)],
        compiler_params=pltpu.CompilerParams(dimension_semantics=('arbitrary', 'arbitrary'), vmem_limit_bytes=40 * 1024 * 1024),
        cost_estimate=pl.CostEstimate(flops=4 * n_stage * rows * width * width * n_model, bytes_accessed=2 * new.size, transcendentals=n_stage * n_model * rows * width),
        name='forward',
    )(acts, new, new)


def solution(mesh):
    n_stage = mesh.shape['stage']
    n_data = mesh.shape['data']
    n_model = mesh.shape['model']
    swap = [(0, 1), (1, 0)]
    up_spec = P('stage', None, 'model')
    down_spec = P('stage', 'model', None)
    row_spec = P(None, 'data', None)
    in_specs = (up_spec, down_spec, up_spec, down_spec, up_spec, down_spec, P('data', 'stage', None, 'model'), P('data', 'stage', 'model', None), P('stage', 'data', None), P('data', None), row_spec, P(None), P(None))
    out_specs = (up_spec, down_spec, up_spec, down_spec, up_spec, down_spec, row_spec)

    def device_step(w_up, w_down, m_up, m_down, v_up, v_down, g_up, g_down, acts_last, grad_out, x_next, learn_rate, max_norm):
        stage_id = lax.axis_index('stage')
        model_id = lax.axis_index('model')
        data_id = lax.axis_index('data')
        acts_in = acts_last[0]
        w_up, w_down, m_up, m_down, v_up, v_down = (t[0] for t in (w_up, w_down, m_up, m_down, v_up, v_down))
        g_up, g_down = g_up[0, 0], g_down[0, 0]
        d_model, ff_local = w_up.shape
        half = d_model // n_data
        up_bf = w_up.astype(BF16)
        down_bf = w_down.astype(BF16)

        def half_of(arr, which):
            return lax.dynamic_slice_in_dim(arr, which * half, half, 0)

        own = jnp.stack([up_bf, down_bf]).reshape(2, n_data, half, d_model)
        mean, norm_tile = backward_all(own, acts_in, grad_out, g_up, g_down, n_stage, n_data, n_model)
        mean_up, mean_down = mean[0], mean[1]
        norm_sq = jnp.sum(norm_tile)
        clip = jnp.minimum(1.0, max_norm[0] / (jnp.sqrt(norm_sq) + NORM_EPS))
        step_rate = learn_rate[0]

        up_half = adamw_update(half_of(w_up, data_id), half_of(m_up, data_id), half_of(v_up, data_id), clip * mean_up, step_rate)[0]
        down_half = adamw_update(half_of(w_down, data_id), half_of(m_down, data_id), half_of(v_down, data_id), clip * mean_down, step_rate)[0]
        new = gather_weights(jnp.stack([up_half.astype(BF16), down_half.astype(BF16)]), n_stage, n_model, n_data)

        new, mean_up, mean_down = lax.optimization_barrier((new, mean_up, mean_down))
        other_up = lax.ppermute(mean_up, 'data', swap)
        other_down = lax.ppermute(mean_down, 'data', swap)

        def join(mine, other):
            first = jnp.where(data_id == 0, mine, other)
            second = jnp.where(data_id == 0, other, mine)
            return jnp.concatenate([first, second], axis=0)

        up_w, up_m, up_v = adamw_update(w_up, m_up, v_up, clip * join(mean_up, other_up), step_rate)
        down_w, down_m, down_v = adamw_update(w_down, m_down, v_down, clip * join(mean_down, other_down), step_rate)

        acts_cur = lax.dynamic_index_in_dim(x_next, stage_id * n_model + model_id, 0, keepdims=False)
        y_next = store_out(gather_out(forward_rows(acts_cur, new), n_stage, n_model))
        return (up_w[None], down_w[None], up_m[None], down_m[None], up_v[None], down_v[None], y_next)

    return jax.shard_map(device_step, mesh=mesh, in_specs=in_specs, out_specs=out_specs, check_vma=False)
```

time: 668 us -> 595 us (0.89)
  waiting for transfers between devices: 35.5 us -> 0.01 us
  local copies, waits for them, and re-layouts: 34.1 us -> 3.39 us
  Pallas kernels: 541 us -> 564 us
  matrix products: 18.2 us -> 0 us
  other arithmetic: 31.8 us -> 22.3 us
    pallas_call x3, Pallas kernels: 312 us -> 355 us  [the longest x1 213 us: backward_all(): pl.pallas_call(functools.partial(chain_kernel, n_stage, n_data, n_model),...]
    ppermute x2 -> x0, waiting for transfers between devices: 35.4 us -> none  [the longest x1 18.6 us: device_step(): got_down = lax.ppermute(half_of(sum_down, 1 - data_id), 'data', swap)]
    unnamed x29 -> x14, local copies, waits for them, and re-layouts: 27.7 us -> 1.88 us
    pallas_call x1, Pallas kernels: 67.2 us -> 46.8 us  [forward_rows(): pl.pallas_call(functools.partial(mlp_kernel, 256), out_shape=jax.ShapeDty...]
    dot_general x3 -> x0, matrix products: 18.2 us -> none  [the longest x2 13.9 us: dot(): return lax.dot_general(left, right, dims, preferred_element_type=F32)]
  transfers between devices with their start and end apart: 4 -> 2, of which waited for: 2 -> 0; matrix products, arithmetic and copies ran while one was open for 1% -> 1% of each run, Pallas kernels for 32% -> 32%
where the time goes in v2:
time: 595 us
  Pallas kernels  564 us (95%)
  other arithmetic  22.3 us (4%)
    pallas_call x1, Pallas kernels, backward_all(): pl.pallas_call(functools.partial(chain_kernel, n_stage, n_data, n_model),...  213 us
    pallas_call x1, Pallas kernels, gather_weights(): pl.pallas_call(functools.partial(weights_kernel, n_model), out_shape=jax....  162 us
    pallas_call x1, Pallas kernels, gather_out(): pl.pallas_call(functools.partial(out_kernel, n_model, pieces), out_shape=...  133 us
    pallas_call x1, Pallas kernels, forward_rows(): pl.pallas_call(functools.partial(mlp_kernel, 256), out_shape=jax.ShapeDty...  46.8 us
  transfers between devices with their start and end apart: 2, of which 0 were waited for; matrix products, arithmetic and copies ran while one was open for 1% of the time, Pallas kernels for 32%

profile of v2, /device:TPU:0, one launch (start us, length us, event | category | flops | bytes accessed | tf_op | source)
XLA Modules:
  0.0 594.6 jit_solution(7651630025713414252)
XLA Ops:
  0.6 0.0 copy-start
  0.6 1.9 convert_element_type.16
  2.6 0.4 copy-done
  3.0 0.1 convert_element_type.17
  3.1 1.6 pad_maximum_fusion.own
  4.7 213.0 %backward.1 = (f32[2,384,768]{2,1,0:T(8,128)}, f32[8,128]{1,0:T(8,128)}) custom-call(bf16[2,2,384,768]{3,2,1,0:T(8,128)(2,1)} %pad_maximum_fusion.own, bf16[1024,768]{1,0:T(8,128)(2,1)} %bitcast.28, bf16[1024,768]{1,0:T(8,128)(2,1)} %grad.1, f32[768,768]{1,0:T(8,128)} %bitcast.26, f32[768,768]{1,0:T(8,128)} %bitcast.27), custom_call_target="tpu_custom_call" | custom-call | tf_op jit(solution)/shard_map/backward/pallas_call | solution.py:266
  217.8 1.3 reduce_sum.9
  221.1 6.3 %slice_bitcast_fusion = (f32[384,768]{1,0:T(8,128)S(1)}, f32[384,768]{1,0:T(8,128)}, bf16[1,384,768]{2,1,0:T(8,128)(2,1)S(1)}, bf16[1,384,768]{2,1,0:T(8,128)(2,1)S(1)}) fusion(f32[2,384,768]{2,1,0:T(8,128)} %get-tuple-element.13, f32[1,768,768]{2,1,0:T(8,128)} %param.18, s32[]{:T(128)S(6)} %select_n.33, f32[]{:T(128)S(6)} %min_shard_map.3, ...), kind=kLoop, calls=%fused_computation.33 | loop fusion | flops 10027008 | bytes 12976140 | tf_op jit(solution)/shard_map/squeeze | solution.py:626
  227.4 1.1 pad_maximum_fusion.1.own
  228.5 162.0 %weights.1.up.down = bf16[4,4,2,2,384,768]{5,4,3,2,1,0:T(8,128)(2,1)} custom-call(bf16[2,384,768]{2,1,0:T(8,128)(2,1)} %pad_maximum_fusion.1.own), custom_call_target="tpu_custom_call" | custom-call | tf_op jit(solution)/shard_map/weights/pallas_call | solution.py:392
  390.6 0.7 collective-permute-start
  391.3 1.4 collective-permute-start.1
  392.7 1.5 dynamic-slice_bitcast_fusion.acts
  394.2 46.8 %forward.1.own = bf16[1024,768]{1,0:T(8,128)(2,1)S(1)} custom-call(bf16[1024,768]{1,0:T(8,128)(2,1)S(1)} %dynamic-slice_bitcast_fusion.acts, bf16[4,4,2,2,384,768]{5,4,3,2,1,0:T(8,128)(2,1)} %weights.1.up.down, bf16[4,4,2,2,384,768]{5,4,3,2,1,0:T(8,128)(2,1)} %weights.1.up.down), custom_call_target="tpu_custom_call" | custom-call | flops 38654705664 | bytes 37748736 | tf_op jit(solution)/shard_map/forward/pallas_call | solution.py:585
  441.0 132.6 %gather_out.1.src = bf16[16,1024,768]{2,1,0:T(8,128)(2,1)S(1)} custom-call(bf16[1024,768]{1,0:T(8,128)(2,1)S(1)} %forward.1.own), custom_call_target="tpu_custom_call" | custom-call | tf_op jit(solution)/shard_map/gather_out/pallas_call | solution.py:508
  573.6 0.0 copy-start.5
  573.6 0.0 copy-start.6
  573.6 9.5 %store_out.1 = bf16[16,1024,768]{2,1,0:T(8,128)(2,1)} custom-call(bf16[16,1024,768]{2,1,0:T(8,128)(2,1)S(1)} %gather_out.1.src), custom_call_target="tpu_custom_call" | custom-call | tf_op jit(solution)/shard_map/store_out/pallas_call | solution.py:533
  583.2 0.0 collective-permute-done
  583.2 0.0 copy-start.3
  583.2 0.0 copy-start.4
  583.2 1.9 select_bitcast_fusion.3
  585.1 0.0 copy-start.1
  585.2 0.0 copy-start.2
  585.2 0.0 collective-permute-done.1
  585.2 1.6 select_bitcast_fusion.1
  586.8 0.0 copy-done.5
  586.8 0.0 copy-done.6
  586.8 0.0 copy-done.3
  586.8 0.7 copy-done.1
  587.6 0.7 copy-done.2
  588.3 6.4 %multiply_subtract_fusion = (f32[1,768,768]{2,1,0:T(8,128)}, f32[1,768,768]{2,1,0:T(8,128)}, f32[1,768,768]{2,1,0:T(8,128)}, f32[1,768,768]{2,1,0:T(8,128)}, f32[1,768,768]{2,1,0:T(8,128)}, /*index=5*/f32[1,768,768]{2,1,0:T(8,128)}) fusion(f32[1,768,768]{2,1,0:T(8,128)S(1)} %copy-done.1, f32[]{:T(128)} %bitcast.21, f32[1,384,768]{2,1,0:T(8,128)S(1)} %get-tuple-element.24, ...), kind=kLoop, calls=%fused_computation.7 | loop fusion | flops 20054016 | bytes 33030152 | tf_op jit(solution)/shard_map/sub | solution.py:28
  (1 shorter events, 0.0 us)
Async XLA Ops:
  0.6 2.4 copy-start
  390.6 192.6 %collective-permute-start = (f32[384,768]{1,0:T(8,128)}, f32[384,768]{1,0:T(8,128)}, u32[]{:S(2)}, u32[]{:S(2)}) collective-permute-start(f32[384,768]{1,0:T(8,128)} %get-tuple-element.14), channel_id=1, source_target_pairs={{0,4},{4,0},{1,5},{5,1},{2,6},{6,2},{3,7},{7,3},{8,12},{12,8},{9,1... | collective-permute-start | bytes 3538952 | tf_op jit(solution)/shard_map/ppermute | solution.py:636
  391.3 193.9 %collective-permute-start.1 = (f32[384,768]{1,0:T(8,128)S(1)}, f32[384,768]{1,0:T(8,128)}, u32[]{:S(2)}, u32[]{:S(2)}) collective-permute-start(f32[384,768]{1,0:T(8,128)S(1)} %get-tuple-element.15), channel_id=1, source_target_pairs={{0,4},{4,0},{1,5},{5,1},{2,6},{6,2},{3,7},{7,3},{8,12},{12,8},{9,1... | collective-permute-start | bytes 3538952 | tf_op jit(solution)/shard_map/ppermute | solution.py:637
  573.6 13.2 %copy-start.5 = (f32[1,768,768]{2,1,0:T(8,128)S(1)}, f32[1,768,768]{2,1,0:T(8,128)}, u32[]{:S(2)}) copy-start(f32[1,768,768]{2,1,0:T(8,128)} %param.17) | copy-start | bytes 7077892
  573.6 13.2 %copy-start.6 = (f32[1,768,768]{2,1,0:T(8,128)S(1)}, f32[1,768,768]{2,1,0:T(8,128)}, u32[]{:S(2)}) copy-start(f32[1,768,768]{2,1,0:T(8,128)} %param.15) | copy-start | bytes 7077892
  583.2 3.6 copy-start.3
  583.2 3.6 copy-start.4
  585.1 2.4 copy-start.1
  585.2 3.1 copy-start.2

commit v3 on v2

--- a/solution.py
+++ b/solution.py
@@ -78,29 +78,44 @@
     return pre_act * cdf, slope
 
 
-def chain_kernel(n_stage, n_data, n_model, own, acts, grad, g_up, g_down, mean, norm, wfull, slopes, gbuf, obuf, gathered, hid, slope, dz, sbuf, rbuf, part, slots,
-                 wsend, wrecv, ysend, yrecv, gsend, grecv, csend, crecv, rsend, rrecv, nsend, nrecv):
+PER_MAT = 2
+
+
+def chain_kernel(n_stage, n_data, n_model, own, acts_in, grad_in, g_up_in, g_down_in, mean, norm, acts, grad, g_up, g_down, wfull, slopes, gbuf, obuf, gathered, hid, slope, dz, sbuf, rbuf, part, slots,
+                 wsend, wrecv, ysend, yrecv, gsend, grecv, dsend, csend, crecv, rsend, rrecv, nsend, nrecv, isem):
     net = Net()
     z, y, s = net.z, net.y, net.s
     half, width = own.shape[2], own.shape[3]
     few = gbuf.shape[0]
 
-    def z_copy(zs, mat, up, src):
+    n_piece = 2 * PER_MAT
+    step = half // PER_MAT
+
+    def full_piece(zs, ys, q):
+        return wfull.at[zs, ys, q // PER_MAT, pl.ds(q % PER_MAT * step, step)]
+
+    def z_copy(zs, q, up, src=None):
         to = z + 1 if up else z - 1
-        return net.send(src, wfull.at[zs, y, mat], wsend.at[int(up), zs, mat], wrecv.at[zs, mat], {'model': to})
-
-    def y_copy(zs, mat, ys):
-        return net.send(wfull.at[zs, ys, mat], wfull.at[zs, ys, mat], ysend.at[zs, mat], yrecv.at[zs, mat], {'data': net.y_other})
+        src = full_piece(zs, y, q) if src is None else src
+        return net.send(src, full_piece(zs, y, q), wsend.at[int(up), zs, q], wrecv.at[zs, q], {'model': to})
+
+    def y_copy(zs, q, ys):
+        return net.send(full_piece(zs, ys, q), full_piece(zs, ys, q), ysend.at[zs, q], yrecv.at[zs, q], {'data': net.y_other})
 
     def has_room(up):
         return (z < n_model - 1) if up else (z > 0)
 
-    for mat in range(2):
+    for q in range(n_piece):
         for up in (False, True):
-            when_all([has_room(up)], lambda: z_copy(z, mat, up, own.at[mat, y]).start())
+            when_all([has_room(up)], lambda: z_copy(z, q, up, own.at[q // PER_MAT, y, pl.ds(q % PER_MAT * step, step)]).start())
+    inputs = [pltpu.make_async_copy(src, dst, isem.at[k]) for k, (src, dst) in enumerate(((acts_in, acts), (grad_in, grad), (g_up_in, g_up), (g_down_in, g_down)))]
+    for copy in inputs:
+        copy.start()
     for mat in range(2):
         for h in range(2):
             wfull[z, h, mat] = own[mat, h]
+    for copy in inputs:
+        copy.wait()
 
     up_own = own[0].reshape(2 * half, width)
     down_own = own[1].reshape(2 * half, width)
@@ -117,20 +132,20 @@
     lax.fori_loop(0, n_model, local_body, 0)
 
     for d in range(1, n_model):
-        for mat in range(2):
+        for q in range(n_piece):
             for side in range(2):
                 zs, ok = side_of(z, n_model, d, side)
                 up = side == 0
                 def take():
-                    z_copy(zs, mat, up, wfull.at[zs, y, mat]).wait_recv()
-                    y_copy(zs, mat, y).start()
+                    z_copy(zs, q, up).wait_recv()
+                    y_copy(zs, q, y).start()
                 when_all([ok], take)
-                when_all([ok, has_room(up)], lambda: z_copy(zs, mat, up, wfull.at[zs, y, mat]).start())
+                when_all([ok, has_room(up)], lambda: z_copy(zs, q, up).start())
     for d in range(1, n_model):
-        for mat in range(2):
+        for q in range(n_piece):
             for side in range(2):
                 zs, ok = side_of(z, n_model, d, side)
-                when_all([ok], lambda: y_copy(zs, mat, net.y_other).wait_recv())
+                when_all([ok], lambda: y_copy(zs, q, net.y_other).wait_recv())
 
     def pre_body(j, _):
         slopes[j] = gelu_parts(dot(acts[rows_at(z), :], wfull[j, :, 0].reshape(2 * half, width)))[1]
@@ -148,9 +163,24 @@
     def _():
         gbuf[...] = grad[rows_at(z), :]
 
+    def g_push(k):
+        return net.send(gbuf, gathered.at[z], dsend.at[k], grecv.at[z], {'model': lax.rem(z + k, n_model)})
+
+    def g_take(k):
+        zs = lax.rem(z + k, n_model)
+        return net.send(gbuf, gathered.at[zs], dsend.at[k], grecv.at[zs], {'data': net.y_other})
+
     @pl.when(s < n_stage - 1)
     def _():
         g_in.wait_recv()
+
+    @pl.when((s > 0) & (s < n_stage - 1))
+    def _():
+        for k in (2, 1, 3):
+            g_push(k).start()
+
+    @pl.when(s == 0)
+    def _():
         for up in (False, True):
             when_all([has_room(up)], lambda: g_copy(z, up, gbuf).start())
 
@@ -170,7 +200,13 @@
         for k in range(n_model):
             gathered[k] = grad[k * few:(k + 1) * few, :]
 
-    @pl.when(s < n_stage - 1)
+    @pl.when((s > 0) & (s < n_stage - 1))
+    def _():
+        gathered[z] = gbuf[...]
+        for k in range(1, n_model):
+            g_take(k).wait_recv()
+
+    @pl.when(s == 0)
     def _():
         gathered[z] = gbuf[...]
         for d in range(1, n_model):
@@ -241,16 +277,21 @@
             for up in (False, True):
                 if d and up != (side == 0):
                     continue
-                for mat in range(2):
-                    when_all([ok, has_room(up)], lambda: z_copy(zs, mat, up, wfull.at[zs, y, mat]).wait_send())
-                when_all([ok, has_room(up), s < n_stage - 1], lambda: g_copy(zs, up, gathered.at[zs]).wait_send())
+                for q in range(n_piece):
+                    when_all([ok, has_room(up)], lambda: z_copy(zs, q, up).wait_send())
+                when_all([ok, has_room(up), s == 0], lambda: g_copy(zs, up, gathered.at[zs]).wait_send())
             if d:
-                for mat in range(2):
-                    when_all([ok], lambda: y_copy(zs, mat, y).wait_send())
+                for q in range(n_piece):
+                    when_all([ok], lambda: y_copy(zs, q, y).wait_send())
 
     @pl.when(s > 0)
     def _():
         g_in.wait_send()
+
+    @pl.when((s > 0) & (s < n_stage - 1))
+    def _():
+        for k in range(1, n_model):
+            g_push(k).wait_send()
 
 
 VMEM_SPEC = pl.BlockSpec(memory_space=pltpu.VMEM)
@@ -266,9 +307,13 @@
     return pl.pallas_call(
         functools.partial(chain_kernel, n_stage, n_data, n_model),
         out_shape=(jax.ShapeDtypeStruct((2, half, width), F32), jax.ShapeDtypeStruct((8, 128), F32)),
-        in_specs=[VMEM_SPEC] * 5,
+        in_specs=[VMEM_SPEC] + [ANY_SPEC] * 4,
         out_specs=(VMEM_SPEC, VMEM_SPEC),
         scratch_shapes=[
+            pltpu.VMEM((rows, width), BF16),
+            pltpu.VMEM((rows, width), BF16),
+            pltpu.VMEM((2 * half, width), F32),
+            pltpu.VMEM((2 * half, width), F32),
             pltpu.VMEM((n_model, 2, 2, half, width), BF16),
             pltpu.VMEM((n_model, few, 2 * half), F32),
             pltpu.VMEM((few, width), BF16),
@@ -281,8 +326,8 @@
             pltpu.VMEM((2, half, width), F32),
             pltpu.VMEM((8, 128), F32),
             pltpu.VMEM((count, 8, 128), F32),
-            DMA((2, n_model, 2)), DMA((n_model, 2)), DMA((n_model, 2)), DMA((n_model, 2)),
-            DMA((2, n_model)), DMA((n_model,)), DMA((1,)), DMA((1,)), DMA((2,)), DMA((2,)), DMA((count,)), DMA((count,)),
+            DMA((2, n_model, 2 * PER_MAT)), DMA((n_model, 2 * PER_MAT)), DMA((n_model, 2 * PER_MAT)), DMA((n_model, 2 * PER_MAT)),
+            DMA((2, n_model)), DMA((n_model,)), DMA((n_model,)), DMA((1,)), DMA((1,)), DMA((2,)), DMA((2,)), DMA((count,)), DMA((count,)), DMA((4,)),
         ],
         compiler_params=pltpu.CompilerParams(has_side_effects=True, vmem_limit_bytes=60 * 1024 * 1024),
         name='backward',
@@ -403,7 +448,7 @@
     )(own)
 
 
-def out_kernel(n_model, pieces, own, out, zsend, xsend, csend, recv, local):
+def out_kernel(n_model, pieces, groups, acts, new, out, own, total, wbuf, wsem, zsend, xsend, csend, recv, local):
     net = Net()
     z, s = net.z, net.s
     last = len(pieces) - 1
@@ -464,12 +509,54 @@
                 when_all([ok], lambda: arrive(net.s_across, zs, part))
                 across(d, side, part, start)
 
+    n_block = new.shape[0] * n_model
+    width = own.shape[1]
+    few = 128
+
+    def fetch(t):
+        slot_of = lax.rem(t, 2)
+        return pltpu.make_async_copy(new.at[lax.rem(t, n_block) // n_model, lax.rem(t, n_model)], wbuf.at[slot_of], wsem.at[slot_of])
+
+    own[...] = acts[...]
+    fetch(0).start()
+    for n, (base, count, ready) in enumerate(groups):
+        def block(t, _, base=base, count=count):
+            fetch(t).wait()
+
+            @pl.when(t + 1 < n_block * len(groups))
+            def _():
+                fetch(t + 1).start()
+
+            turn = lax.rem(t, n_model)
+
+            @pl.when(turn == 0)
+            def _():
+                total[...] = jnp.zeros(total.shape, F32)
+
+            held = wbuf.at[lax.rem(t, 2)]
+            up_w = held[:, 0].reshape(width, width)
+            down_w = held[:, 1].reshape(width, width)
+            ahead = dot(own[base:base + few, :], up_w)
+            for r in range(count // few):
+                pre = ahead
+                if (r + 1) * few < count:
+                    ahead = dot(own[base + (r + 1) * few:base + (r + 2) * few, :], up_w)
+                total[r * few:(r + 1) * few, :] += dot(gelu_parts(pre)[0].astype(BF16), down_w)
+
+            @pl.when(turn == n_model - 1)
+            def _():
+                own[base:base + count, :] = (own[base:base + count, :].astype(F32) + total[:count, :]).astype(BF16)
+
+            return 0
+
+        lax.fori_loop(n * n_block, (n + 1) * n_block, block, 0)
+        if last in ready:
+            first = go('x', s, z, last, own.at[parts[last]])
+            first.start()
+        for part in ready:
+            pass_on(s, 0, 0, part, start)
     mine = pltpu.make_async_copy(own, out.at[s * n_model + z], local.at[0])
     mine.start()
-    first = go('x', s, z, last, own.at[parts[last]])
-    first.start()
-    for part in range(last + 1):
-        pass_on(s, 0, 0, part, start)
     arrive(net.s_across, z, last)
     pass_on(net.s_across, 0, 0, last, start)
     for d in range(1, n_model):
@@ -500,23 +587,26 @@
     mine.wait()
 
 
-def gather_out(own, n_stage, n_model):
-    rows, width = own.shape
+def forward_out(acts, new):
+    n_stage, n_model, n_data, n_mat, half, width = new.shape
+    rows = acts.shape[0]
     unit = rows // 64
-    pieces = ((0, 19 * unit), (19 * unit, 19 * unit), (38 * unit, 18 * unit), (56 * unit, 8 * unit))
+    pieces = ((8 * unit, 12 * unit), (20 * unit, 12 * unit), (32 * unit, 16 * unit), (48 * unit, 16 * unit), (0, 8 * unit))
+    groups = ((0, rows // 2, (4, 0, 1)), (rows // 2, rows // 2, (2, 3)))
     n_part = len(pieces)
     return pl.pallas_call(
-        functools.partial(out_kernel, n_model, pieces),
+        functools.partial(out_kernel, n_model, pieces, groups),
         out_shape=jax.ShapeDtypeStruct((n_stage * n_model, rows, width), BF16),
-        in_specs=[VMEM_SPEC],
+        in_specs=[VMEM_SPEC, ANY_SPEC],
         out_specs=ANY_SPEC,
         scratch_shapes=[
+            pltpu.VMEM((rows, width), BF16), pltpu.VMEM((rows // 2, width), F32), pltpu.VMEM((2, n_data, n_mat, half, width), BF16), DMA((2,)),
             DMA((2, 2, n_model, n_part)), DMA((n_model, n_part)), DMA((2, n_model, n_part)),
             DMA((n_stage, n_model, n_part)), DMA((1,)),
         ],
-        compiler_params=pltpu.CompilerParams(has_side_effects=True, vmem_limit_bytes=4 * 1024 * 1024),
-        name='gather_out',
-    )(own)
+        compiler_params=pltpu.CompilerParams(has_side_effects=True, vmem_limit_bytes=20 * 1024 * 1024),
+        name='forward_out',
+    )(acts, new)
 
 
 def store_kernel(src, dst, sems):
@@ -539,60 +629,6 @@
         compiler_params=pltpu.CompilerParams(vmem_limit_bytes=4 * 1024 * 1024),
         name='store_out',
     )(rows)
-
-
-def mlp_kernel(rows_step, acts, up, down, out, cur, total):
-    p, j = pl.program_id(0), pl.program_id(1)
-    rows, width = cur.shape
-
-    @pl.when((p == 0) & (j == 0))
-    def _():
-        cur[...] = acts[...]
-
-    @pl.when(j == 0)
-    def _():
-        total[...] = jnp.zeros(total.shape, F32)
-
-    up_w = up[0, 0, :, 0].reshape(width, width)
-    down_w = down[0, 0, :, 0].reshape(width, width)
-    n_step = rows // rows_step
-
-    def at(r):
-        return pl.ds(r * rows_step, rows_step)
-
-    ahead = dot(cur[at(0), :], up_w)
-    for r in range(n_step):
-        pre = ahead
-        if r + 1 < n_step:
-            ahead = dot(cur[at(r + 1), :], up_w)
-        total[at(r), :] += dot(gelu_parts(pre)[0].astype(BF16), down_w)
-
-    @pl.when(j == pl.num_programs(1) - 1)
-    def _():
-        cur[...] = (cur[...].astype(F32) + total[...]).astype(BF16)
-
-    @pl.when((p == pl.num_programs(0) - 1) & (j == pl.num_programs(1) - 1))
-    def _():
-        out[...] = cur[...]
-
-
-def forward_rows(acts, new):
-    n_stage, n_model, n_data, _, half, width = new.shape
-    rows = acts.shape[0]
-    def spec(mat):
-        return pl.BlockSpec((1, 1, n_data, 1, half, width), lambda p, j: (p, j, 0, mat, 0, 0))
-    whole = pl.BlockSpec((rows, width), lambda p, j: (0, 0))
-    return pl.pallas_call(
-        functools.partial(mlp_kernel, 256),
-        out_shape=jax.ShapeDtypeStruct((rows, width), BF16),
-        grid=(n_stage, n_model),
-        in_specs=[whole, spec(0), spec(1)],
-        out_specs=whole,
-        scratch_shapes=[pltpu.VMEM((rows, width), BF16), pltpu.VMEM((rows, width), F32)],
-        compiler_params=pltpu.CompilerParams(dimension_semantics=('arbitrary', 'arbitrary'), vmem_limit_bytes=40 * 1024 * 1024),
-        cost_estimate=pl.CostEstimate(flops=4 * n_stage * rows * width * width * n_model, bytes_accessed=2 * new.size, transcendentals=n_stage * n_model * rows * width),
-        name='forward',
-    )(acts, new, new)
 
 
 def solution(mesh):
@@ -645,7 +681,7 @@
         down_w, down_m, down_v = adamw_update(w_down, m_down, v_down, clip * join(mean_down, other_down), step_rate)
 
         acts_cur = lax.dynamic_index_in_dim(x_next, stage_id * n_model + model_id, 0, keepdims=False)
-        y_next = store_out(gather_out(forward_rows(acts_cur, new), n_stage, n_model))
+        y_next = store_out(forward_out(acts_cur, new))
         return (up_w[None], down_w[None], up_m[None], down_m[None], up_v[None], down_v[None], y_next)
 
     return jax.shard_map(device_step, mesh=mesh, in_specs=in_specs, out_specs=out_specs, check_vma=False)

time: 595 us -> 575 us (0.966)
  Pallas kernels: 564 us -> 544 us
    pallas_call x1, Pallas kernels: 213 us -> 202 us  [backward_all(): pl.pallas_call(functools.partial(chain_kernel, n_stage, n_data, n_model),...]
    pallas_call x2 -> x1, Pallas kernels: 179 us -> 171 us  [forward_out(): pl.pallas_call(functools.partial(out_kernel, n_model, pieces, groups), ou...]
  transfers between devices with their start and end apart: 2 -> 2, of which waited for: 0 -> 0; matrix products, arithmetic and copies ran while one was open for 1% -> 1% of each run, Pallas kernels for 32% -> 31%
where the time goes in v3:
time: 575 us; the launch traced here: 574 us
  Pallas kernels  544 us (95%)
  other arithmetic  21.8 us (4%)
    pallas_call x1, Pallas kernels, backward_all(): pl.pallas_call(functools.partial(chain_kernel, n_stage, n_data, n_model),...  202 us
    pallas_call x1, Pallas kernels, forward_out(): pl.pallas_call(functools.partial(out_kernel, n_model, pieces, groups), ou...  171 us
    pallas_call x1, Pallas kernels, gather_weights(): pl.pallas_call(functools.partial(weights_kernel, n_model), out_shape=jax....  162 us
  transfers between devices with their start and end apart: 2, of which 0 were waited for; matrix products, arithmetic and copies ran while one was open for 1% of the time, Pallas kernels for 31%

profile of v3, /device:TPU:0, one launch (start us, length us, event | category | flops | bytes accessed | tf_op | source)
XLA Modules:
  0.0 573.8 jit_solution(6096105989288263326)
XLA Ops:
  0.6 0.0 copy-start
  2.1 1.8 convert_element_type.16
  3.9 0.0 copy-done
  3.9 0.1 convert_element_type.17
  4.0 1.6 pad_maximum_fusion.own
  5.6 202.4 %backward.1 = (f32[2,384,768]{2,1,0:T(8,128)}, f32[8,128]{1,0:T(8,128)}) custom-call(bf16[2,2,384,768]{3,2,1,0:T(8,128)(2,1)} %pad_maximum_fusion.own, bf16[1024,768]{1,0:T(8,128)(2,1)} %bitcast.28, bf16[1024,768]{1,0:T(8,128)(2,1)} %grad_in.1, f32[768,768]{1,0:T(8,128)} %bitcast.26, f32[768,768]{1,0:T(8,128)} %bitcast.27), custom_call_target="tpu_custom_call" | custom-call | tf_op jit(solution)/shard_map/backward/pallas_call | solution.py:307
  208.0 1.3 reduce_sum.9
  210.0 6.3 %slice_bitcast_fusion = (f32[384,768]{1,0:T(8,128)S(1)}, f32[384,768]{1,0:T(8,128)}, bf16[1,384,768]{2,1,0:T(8,128)(2,1)S(1)}, bf16[1,384,768]{2,1,0:T(8,128)(2,1)S(1)}) fusion(f32[2,384,768]{2,1,0:T(8,128)} %get-tuple-element.13, f32[1,768,768]{2,1,0:T(8,128)} %param.18, s32[]{:T(128)S(6)} %select_n.33, f32[]{:T(128)S(6)} %min_shard_map.3, ...), kind=kLoop, calls=%fused_computation.33 | loop fusion | flops 10027008 | bytes 12976140 | tf_op jit(solution)/shard_map/squeeze | solution.py:662
  216.4 1.1 pad_maximum_fusion.1.own
  217.5 161.7 %weights.1.new = bf16[4,4,2,2,384,768]{5,4,3,2,1,0:T(8,128)(2,1)} custom-call(bf16[2,384,768]{2,1,0:T(8,128)(2,1)} %pad_maximum_fusion.1.own), custom_call_target="tpu_custom_call" | custom-call | tf_op jit(solution)/shard_map/weights/pallas_call | solution.py:437
  379.2 0.7 collective-permute-start
  379.9 1.4 collective-permute-start.1
  381.3 1.5 dynamic-slice_bitcast_fusion.acts
  382.8 170.8 %forward_out.1.src = bf16[16,1024,768]{2,1,0:T(8,128)(2,1)S(1)} custom-call(bf16[1024,768]{1,0:T(8,128)(2,1)S(1)} %dynamic-slice_bitcast_fusion.acts, bf16[4,4,2,2,384,768]{5,4,3,2,1,0:T(8,128)(2,1)} %weights.1.new), custom_call_target="tpu_custom_call" | custom-call | tf_op jit(solution)/shard_map/forward_out/pallas_call | solution.py:597
  553.6 0.0 copy-start.6
  553.6 0.0 copy-start.5
  553.6 9.1 %store_out.1 = bf16[16,1024,768]{2,1,0:T(8,128)(2,1)} custom-call(bf16[16,1024,768]{2,1,0:T(8,128)(2,1)S(1)} %forward_out.1.src), custom_call_target="tpu_custom_call" | custom-call | tf_op jit(solution)/shard_map/store_out/pallas_call | solution.py:623
  562.7 0.0 collective-permute-done
  562.8 0.0 copy-done.6
  562.8 0.0 copy-start.3
  562.8 0.0 copy-start.4
  562.8 1.6 select_bitcast_fusion.3
  564.4 0.0 copy-start.1
  564.4 0.0 copy-start.2
  564.4 0.0 collective-permute-done.1
  564.4 1.6 select_bitcast_fusion.1
  566.0 0.0 copy-done.5
  566.0 0.0 copy-done.3
  566.0 0.0 copy-done.4
  566.0 0.8 copy-done.1
  566.8 0.7 copy-done.2
  567.5 6.4 %multiply_subtract_fusion = (f32[1,768,768]{2,1,0:T(8,128)}, f32[1,768,768]{2,1,0:T(8,128)}, f32[1,768,768]{2,1,0:T(8,128)}, f32[1,768,768]{2,1,0:T(8,128)}, f32[1,768,768]{2,1,0:T(8,128)}, /*index=5*/f32[1,768,768]{2,1,0:T(8,128)}) fusion(f32[1,768,768]{2,1,0:T(8,128)S(1)} %copy-done, f32[]{:T(128)} %bitcast.21, f32[1,384,768]{2,1,0:T(8,128)S(1)} %get-tuple-element.24, ...), kind=kLoop, calls=%fused_computation.7 | loop fusion | flops 20054016 | bytes 33030152 | tf_op jit(solution)/shard_map/sub | solution.py:28
Async XLA Ops:
  0.6 3.2 copy-start
  379.2 183.6 %collective-permute-start = (f32[384,768]{1,0:T(8,128)}, f32[384,768]{1,0:T(8,128)}, u32[]{:S(2)}, u32[]{:S(2)}) collective-permute-start(f32[384,768]{1,0:T(8,128)} %get-tuple-element.14), channel_id=1, source_target_pairs={{0,4},{4,0},{1,5},{5,1},{2,6},{6,2},{3,7},{7,3},{8,12},{12,8},{9,1... | collective-permute-start | bytes 3538952 | tf_op jit(solution)/shard_map/ppermute | solution.py:672
  379.9 184.5 %collective-permute-start.1 = (f32[384,768]{1,0:T(8,128)S(1)}, f32[384,768]{1,0:T(8,128)}, u32[]{:S(2)}, u32[]{:S(2)}) collective-permute-start(f32[384,768]{1,0:T(8,128)S(1)} %get-tuple-element.15), channel_id=1, source_target_pairs={{0,4},{4,0},{1,5},{5,1},{2,6},{6,2},{3,7},{7,3},{8,12},{12,8},{9,1... | collective-permute-start | bytes 3538952 | tf_op jit(solution)/shard_map/ppermute | solution.py:673
  553.6 9.1 %copy-start.6 = (f32[384,768]{1,0:T(8,128)S(1)}, f32[384,768]{1,0:T(8,128)}, u32[]{:S(2)}) copy-start(f32[384,768]{1,0:T(8,128)} %get-tuple-element.14) | copy-start | bytes 3538948
  553.6 12.4 %copy-start.5 = (f32[1,768,768]{2,1,0:T(8,128)S(1)}, f32[1,768,768]{2,1,0:T(8,128)}, u32[]{:S(2)}) copy-start(f32[1,768,768]{2,1,0:T(8,128)} %param.15) | copy-start | bytes 7077892
  562.8 3.3 copy-start.3
  562.8 3.3 copy-start.4
  564.4 2.4 copy-start.1
  564.4 3.1 copy-start.2

commit v4 on v3

--- a/solution.py
+++ b/solution.py
@@ -591,8 +591,8 @@
     n_stage, n_model, n_data, n_mat, half, width = new.shape
     rows = acts.shape[0]
     unit = rows // 64
-    pieces = ((8 * unit, 12 * unit), (20 * unit, 12 * unit), (32 * unit, 16 * unit), (48 * unit, 16 * unit), (0, 8 * unit))
-    groups = ((0, rows // 2, (4, 0, 1)), (rows // 2, rows // 2, (2, 3)))
+    pieces = ((8 * unit, 12 * unit), (20 * unit, 12 * unit), (32 * unit, 12 * unit), (44 * unit, 10 * unit), (54 * unit, 10 * unit), (0, 8 * unit))
+    groups = ((0, rows // 2, (5, 0, 1)), (rows // 2, rows // 2, (2, 3, 4)))
     n_part = len(pieces)
     return pl.pallas_call(
         functools.partial(out_kernel, n_model, pieces, groups),

time: 575 us -> 575 us (level)
  no operation moved by 1% of the time
where the time goes in v4:
time: 575 us; the launch traced here: 574 us
  Pallas kernels  544 us (95%)
  other arithmetic  21.8 us (4%)
    pallas_call x1, Pallas kernels, backward_all(): pl.pallas_call(functools.partial(chain_kernel, n_stage, n_data, n_model),...  202 us
    pallas_call x1, Pallas kernels, forward_out(): pl.pallas_call(functools.partial(out_kernel, n_model, pieces, groups), ou...  171 us
    pallas_call x1, Pallas kernels, gather_weights(): pl.pallas_call(functools.partial(weights_kernel, n_model), out_shape=jax....  162 us
  transfers between devices with their start and end apart: 2, of which 0 were waited for; matrix products, arithmetic and copies ran while one was open for 1% of the time, Pallas kernels for 31%

profile of v4, /device:TPU:0, one launch (start us, length us, event | category | flops | bytes accessed | tf_op | source)
XLA Modules:
  0.0 574.0 jit_solution(5357374698221717563)
XLA Ops:
  0.6 0.0 copy-start
  2.1 1.8 convert_element_type.16
  3.9 0.0 copy-done
  3.9 0.1 convert_element_type.17
  4.0 1.6 pad_maximum_fusion.own
  5.6 202.4 %backward.1 = (f32[2,384,768]{2,1,0:T(8,128)}, f32[8,128]{1,0:T(8,128)}) custom-call(bf16[2,2,384,768]{3,2,1,0:T(8,128)(2,1)} %pad_maximum_fusion.own, bf16[1024,768]{1,0:T(8,128)(2,1)} %bitcast.28, bf16[1024,768]{1,0:T(8,128)(2,1)} %grad_in.1, f32[768,768]{1,0:T(8,128)} %bitcast.26, f32[768,768]{1,0:T(8,128)} %bitcast.27), custom_call_target="tpu_custom_call" | custom-call | tf_op jit(solution)/shard_map/backward/pallas_call | solution.py:307
  208.0 1.3 reduce_sum.9
  210.0 6.3 %slice_bitcast_fusion = (f32[384,768]{1,0:T(8,128)S(1)}, f32[384,768]{1,0:T(8,128)}, bf16[1,384,768]{2,1,0:T(8,128)(2,1)S(1)}, bf16[1,384,768]{2,1,0:T(8,128)(2,1)S(1)}) fusion(f32[2,384,768]{2,1,0:T(8,128)} %get-tuple-element.13, f32[1,768,768]{2,1,0:T(8,128)} %param.18, s32[]{:T(128)S(6)} %select_n.33, f32[]{:T(128)S(6)} %min_shard_map.3, ...), kind=kLoop, calls=%fused_computation.33 | loop fusion | flops 10027008 | bytes 12976140 | tf_op jit(solution)/shard_map/squeeze | solution.py:662
  216.4 1.1 pad_maximum_fusion.1.own
  217.5 161.7 %weights.1.new = bf16[4,4,2,2,384,768]{5,4,3,2,1,0:T(8,128)(2,1)} custom-call(bf16[2,384,768]{2,1,0:T(8,128)(2,1)} %pad_maximum_fusion.1.own), custom_call_target="tpu_custom_call" | custom-call | tf_op jit(solution)/shard_map/weights/pallas_call | solution.py:437
  379.2 0.7 collective-permute-start
  379.9 1.4 collective-permute-start.1
  381.3 1.5 dynamic-slice_bitcast_fusion.acts
  382.8 171.0 %forward_out.1.src = bf16[16,1024,768]{2,1,0:T(8,128)(2,1)S(1)} custom-call(bf16[1024,768]{1,0:T(8,128)(2,1)S(1)} %dynamic-slice_bitcast_fusion.acts, bf16[4,4,2,2,384,768]{5,4,3,2,1,0:T(8,128)(2,1)} %weights.1.new), custom_call_target="tpu_custom_call" | custom-call | tf_op jit(solution)/shard_map/forward_out/pallas_call | solution.py:597
  553.8 0.0 copy-start.6
  553.8 0.0 copy-start.5
  553.8 9.1 %store_out.1 = bf16[16,1024,768]{2,1,0:T(8,128)(2,1)} custom-call(bf16[16,1024,768]{2,1,0:T(8,128)(2,1)S(1)} %forward_out.1.src), custom_call_target="tpu_custom_call" | custom-call | tf_op jit(solution)/shard_map/store_out/pallas_call | solution.py:623
  562.9 0.0 collective-permute-done
  562.9 0.0 copy-done.6
  562.9 0.0 copy-start.3
  563.0 0.0 copy-start.4
  563.0 1.6 select_bitcast_fusion.3
  564.5 0.0 copy-start.1
  564.6 0.0 copy-start.2
  564.6 0.0 collective-permute-done.1
  564.6 1.6 select_bitcast_fusion.1
  566.2 0.0 copy-done.5
  566.2 0.0 copy-done.3
  566.2 0.0 copy-done.4
  566.2 0.8 copy-done.1
  567.0 0.7 copy-done.2
  567.7 6.4 %multiply_subtract_fusion = (f32[1,768,768]{2,1,0:T(8,128)}, f32[1,768,768]{2,1,0:T(8,128)}, f32[1,768,768]{2,1,0:T(8,128)}, f32[1,768,768]{2,1,0:T(8,128)}, f32[1,768,768]{2,1,0:T(8,128)}, /*index=5*/f32[1,768,768]{2,1,0:T(8,128)}) fusion(f32[1,768,768]{2,1,0:T(8,128)S(1)} %copy-done, f32[]{:T(128)} %bitcast.21, f32[1,384,768]{2,1,0:T(8,128)S(1)} %get-tuple-element.24, ...), kind=kLoop, calls=%fused_computation.7 | loop fusion | flops 20054016 | bytes 33030152 | tf_op jit(solution)/shard_map/sub | solution.py:28
Async XLA Ops:
  0.6 3.2 copy-start
  379.2 183.8 %collective-permute-start = (f32[384,768]{1,0:T(8,128)}, f32[384,768]{1,0:T(8,128)}, u32[]{:S(2)}, u32[]{:S(2)}) collective-permute-start(f32[384,768]{1,0:T(8,128)} %get-tuple-element.14), channel_id=1, source_target_pairs={{0,4},{4,0},{1,5},{5,1},{2,6},{6,2},{3,7},{7,3},{8,12},{12,8},{9,1... | collective-permute-start | bytes 3538952 | tf_op jit(solution)/shard_map/ppermute | solution.py:672
  379.9 184.7 %collective-permute-start.1 = (f32[384,768]{1,0:T(8,128)S(1)}, f32[384,768]{1,0:T(8,128)}, u32[]{:S(2)}, u32[]{:S(2)}) collective-permute-start(f32[384,768]{1,0:T(8,128)S(1)} %get-tuple-element.15), channel_id=1, source_target_pairs={{0,4},{4,0},{1,5},{5,1},{2,6},{6,2},{3,7},{7,3},{8,12},{12,8},{9,1... | collective-permute-start | bytes 3538952 | tf_op jit(solution)/shard_map/ppermute | solution.py:673
  553.8 9.1 %copy-start.6 = (f32[384,768]{1,0:T(8,128)S(1)}, f32[384,768]{1,0:T(8,128)}, u32[]{:S(2)}) copy-start(f32[384,768]{1,0:T(8,128)} %get-tuple-element.14) | copy-start | bytes 3538948
  553.8 12.4 %copy-start.5 = (f32[1,768,768]{2,1,0:T(8,128)S(1)}, f32[1,768,768]{2,1,0:T(8,128)}, u32[]{:S(2)}) copy-start(f32[1,768,768]{2,1,0:T(8,128)} %param.15) | copy-start | bytes 7077892
  562.9 3.3 copy-start.3
  563.0 3.3 copy-start.4
  564.5 2.4 copy-start.1
  564.6 3.1 copy-start.2
